TPU v7x, 256 devices: a whole 4x4x8 slice. The times are simulated.
256 devices in a mesh: gx: 8 (over z_hi, core), gy: 4 (over y), gz: 8 (over z_lo, x).
Axes of the slice: x: 4, y: 4, z: 8 (z_hi: 4, z_lo: 2; z = z_hi * 2 + z_lo), core: 2. Of those that a mesh axis runs over, the one named last changes fastest.
Arguments:
- field: float32 [256, 1024, 512], P('gz', 'gx', 'gy'), may hold values from -48 to 48
- factor_a: float32 [1024, 1024], replicated, may hold values from -0.5 to 3.5
- factor_b: float32 [512, 512], replicated, may hold values from -0.5 to 3.5
- factor_c: float32 [256, 256], replicated, may hold values from -0.5 to 3.5
Outputs:
- propagated: float32 [256, 1024, 512], P('gz', 'gx', 'gy')
All inputs are finite; a program needn't handle non-finite values.
Results may differ from a plain program's by a relative error of at most 0.00007.
Values sent between devices are 32-bit elements; how exact they have to be, the bound alone decides.
No kernel may reach another device: no remote copies, remote signals or barrier semaphores. Data moves between devices by JAX's collectives and lax.ppermute only.
A program may use at most 64 MiB of HBM per device.

v0:
```python
import functools

import jax
import jax.numpy as jnp
from jax import lax
from jax.experimental import pallas as pl
from jax.experimental.pallas import tpu as pltpu
from jax.sharding import Mesh
from jax.sharding import PartitionSpec as P


GX, GZ = ("zh", "core"), ("zl", "x")
Z = ("zh", "zl")
PLANES = ("core", "zh", "zl", "x")

epsilon = 1e-06
target_ratio = 0.5
f32, bf16 = jnp.float32, jnp.bfloat16
LIMIT = pltpu.CompilerParams(vmem_limit_bytes=32 << 20)
HBM = pltpu.HBM
VMEM, SMEM, ANY, IN_HBM = (
    pl.BlockSpec(memory_space=s) for s in (pltpu.VMEM, pltpu.SMEM, pl.ANY, HBM)
)


def halves(x):
    hi = x.astype(bf16)
    return hi, (x - hi.astype(f32)).astype(bf16)


def split_kernel(x_ref, o_ref, *, flip):
    x = x_ref[...]
    hi, lo = halves(x.T if flip else x)
    if flip:
        o_ref[0, 0], o_ref[0, 1] = hi, lo
    else:
        o_ref[0], o_ref[1] = hi, lo


def split_factor(x, flip=0):
    n = x.shape[0]
    step = flip or n
    if flip:
        shape = (n // flip, 2, n, flip)
        out = pl.BlockSpec((1,) + shape[1:], lambda i: (i, 0, 0, 0))
        shape = HBM(shape, bf16)
    else:
        out = pl.BlockSpec((2, n, n), lambda i: (0, 0, 0))
        shape = jax.ShapeDtypeStruct((2, n, n), bf16)
    return pl.pallas_call(
        functools.partial(split_kernel, flip=flip),
        compiler_params=LIMIT,
        grid=(n // step,),
        in_specs=[pl.BlockSpec((step, n), lambda i: (i, 0))],
        out_specs=out,
        out_shape=shape,
    )(x)


def call(kernel, shapes, *args, scratch=(), own=False):
    single = not isinstance(shapes, list)
    shapes = [shapes] if single else shapes
    out = pl.pallas_call(
        kernel,
        compiler_params=LIMIT,
        out_shape=[
            HBM(s, f32) if own and i == 0 else jax.ShapeDtypeStruct(s, f32)
            for i, s in enumerate(shapes)
        ],
        in_specs=[SMEM if a.dtype == jnp.int32 else VMEM for a in args],
        out_specs=[VMEM] * len(shapes),
        scratch_shapes=scratch,
    )(*args)
    return out[0] if single else out


def mm(a, b):
    return jnp.dot(a, b, preferred_element_type=f32)


def left3(a_ref, x):
    hi, lo = halves(x)
    return mm(a_ref[0], hi) + (mm(a_ref[0], lo) + mm(a_ref[1], hi))


def left3_parts(a_ref, hi, lo):
    return mm(a_ref[0], hi) + (mm(a_ref[0], lo) + mm(a_ref[1], hi))


def planes_product(at_ref, c_ref, x_ref, j, along):
    width = at_ref.shape[3]
    m = c_ref.shape[1]
    k = pl.ds(j * m, m)
    lanes = pl.ds(pl.multiple_of(pl.program_id(0) * width, width), width)
    return along[j * m : (j + 1) * m] + left3_parts(c_ref, x_ref[0, k, lanes], x_ref[1, k, lanes])


def along_one(at_ref, x_ref):
    hi, lo = x_ref[0], x_ref[1]
    return mm(hi, at_ref[0, 0]) + (mm(lo, at_ref[0, 0]) + mm(hi, at_ref[0, 1]))


def put(x_ref, j, m, lane, ii, x):
    hi, lo = halves(x.reshape(m, ii))
    x_ref[0, j * m : (j + 1) * m, lane : lane + ii] = hi
    x_ref[1, j * m : (j + 1) * m, lane : lane + ii] = lo


def first_kernel(v_ref, at_ref, c_ref, g_ref, x_ref):
    n_core, n_zh, n_zl, n_x, n_j, kk, ii = v_ref.shape
    n_gy, sub = g_ref.shape[0], g_ref.shape[6]
    m = n_zl * n_x * kk

    @pl.when(pl.program_id(0) == 0)
    def _():
        for j in range(n_j):
            for z in range(n_zh):
                for c in range(n_core):
                    put(x_ref, j, m, (z * n_core + c) * ii, ii, v_ref[c, z, :, :, j])

    along = along_one(at_ref, x_ref)
    for j in range(n_j):
        y = planes_product(at_ref, c_ref, x_ref, j, along)
        for c in range(n_core):
            part = y[:, c * ii : (c + 1) * ii].reshape(n_zl, n_x, n_gy, sub, ii)
            for gy in range(n_gy):
                g_ref[gy, c, 0, :, :, j] = part[:, :, gy]


def second_kernel(g_ref, at_ref, c_ref, h_ref, x_ref):
    n_gy, n_core, n_zh, n_zl, n_x, n_j, sub, ii = g_ref.shape
    m = n_zl * n_x * n_gy * sub

    @pl.when(pl.program_id(0) == 0)
    def _():
        for j in range(n_j):
            for z in range(n_zh):
                for c in range(n_core):
                    x = jnp.stack([g_ref[gy, c, z, :, :, j] for gy in range(n_gy)], axis=2)
                    put(x_ref, j, m, (z * n_core + c) * ii, ii, x)

    along = along_one(at_ref, x_ref)
    for j in range(n_j):
        y = planes_product(at_ref, c_ref, x_ref, j, along)
        for c in range(n_core):
            h_ref[c, 0, :, :, j] = y[:, c * ii : (c + 1) * ii].reshape(n_zl, n_x, n_gy * sub, ii)


def planes_call(kernel, value, at, c, shape):
    zh = len(shape) - 6
    n, m = at.shape[2], c.shape[1]
    n_zh = shape[zh]
    whole = lambda a: pl.BlockSpec(a.shape, lambda i, nd=a.ndim: (0,) * nd)
    index = lambda i: tuple(i if d == zh else 0 for d in range(len(shape)))
    return pl.pallas_call(
        kernel,
        compiler_params=pltpu.CompilerParams(vmem_limit_bytes=61 << 20),
        grid=(n_zh,),
        in_specs=[whole(value), pl.BlockSpec((1,) + at.shape[1:], lambda i: (i, 0, 0, 0)), whole(c)],
        out_specs=pl.BlockSpec(shape[:zh] + (1,) + shape[zh + 1 :], index),
        out_shape=HBM(shape, f32),
        scratch_shapes=[pltpu.VMEM((2, shape[-3] * m, n), bf16)],
    )(value, at, c)


def y_pack_kernel(me_ref, v_ref, *o_refs):
    n_y = len(o_refs)
    sub = v_ref.shape[1] // n_y
    for d, o in enumerate(o_refs):
        to = pl.multiple_of(lax.rem(me_ref[0] + d, n_y) * sub, sub)
        o[...] = v_ref[:, pl.ds(to, sub)]


def square_sum(x):
    return jnp.sum((x * x).reshape(-1, 8, 128), axis=0)


def row_kernel(me_ref, *refs):
    *v_refs, b_ref, o_ref, sum_ref, rows_ref = refs
    gy = len(v_refs)
    for d, v in enumerate(v_refs):
        rows_ref[lax.rem(me_ref[0] + gy - d, gy)] = v[...]
    rows = rows_ref[...]
    sum_ref[...] = square_sum(rows)
    o_ref[...] = left3(b_ref, rows.reshape(gy * rows.shape[1], -1)).reshape(o_ref.shape)


def term_kernel(me_ref, bv_ref, g_ref, *refs):
    *o_refs, sum_ref = refs
    gy = len(o_refs)
    total = jnp.zeros(sum_ref.shape, f32)
    for d, o in enumerate(o_refs):
        to = lax.rem(me_ref[0] + d, gy)
        value = bv_ref[to] + g_ref[to]
        total += square_sum(value)
        o[...] = value
    sum_ref[...] = total


def cross_kernel(me_ref, bv_ref, g_ref, b_ref, *o_refs):
    gy, cols = bv_ref.shape[:2]
    hi, lo = halves((bv_ref[...] + 2.0 * g_ref[...]).reshape(gy * cols, -1))
    for d, o in enumerate(o_refs):
        to = pl.multiple_of(lax.rem(me_ref[0] + d, gy) * cols, cols)
        bh, bl = b_ref[0, pl.ds(to, cols)], b_ref[1, pl.ds(to, cols)]
        o[...] = (mm(bh, hi) + (mm(bh, lo) + mm(bl, hi))).reshape(o.shape)


def last_kernel(me_ref, sum_ref, v_ref, h_ref, *refs):
    n_y = (len(refs) - 7) // 2
    pieces, o_ref = refs[: 2 * n_y], refs[2 * n_y]
    v_buf, h_buf, p_buf, o_buf, in_sem, out_sem = refs[2 * n_y + 1 :]
    sub = v_buf.shape[1]
    loads, stores = [], []
    for d in range(n_y):
        k = pl.ds(pl.multiple_of(lax.rem(me_ref[0] + n_y - d, n_y) * sub, sub), sub)
        parts = (
            (pieces[d], p_buf.at[d, 0]),
            (pieces[n_y + d], p_buf.at[d, 1]),
            (v_ref.at[k], v_buf.at[d]),
            (h_ref.at[:, k], h_buf.at[d]),
        )
        loads.append(
            [pltpu.make_async_copy(a, b, in_sem.at[d, i]) for i, (a, b) in enumerate(parts)]
        )
        stores.append(pltpu.make_async_copy(o_buf.at[d], o_ref.at[k], out_sem.at[d]))
        for load in loads[-1]:
            load.start()
    size_field, size_first = jnp.sum(sum_ref[0]), jnp.sum(sum_ref[1])
    ratio = size_field / (jnp.full((1, 128), size_first, f32) + epsilon)
    step = (target_ratio * jnp.sqrt(ratio)).reshape(1, 1, 128)
    for d in range(n_y):
        for load in loads[d]:
            load.wait()
        value = (step * step / 2.0) * (p_buf[d, 1] + h_buf[d]) - step * p_buf[d, 0]
        for k in range(sub):
            o_buf[d, k] = v_buf[d, k] + value[:, k].T
        stores[d].start()
    for store in stores:
        store.wait()


def last_step(me, sums, field, h, firsts, crosses):
    n_y = len(crosses)
    depth, rows, cols = field.shape
    sub = depth // n_y
    block, turned = (n_y, sub, rows, cols), (n_y, cols, sub, rows)
    return pl.pallas_call(
        last_kernel,
        compiler_params=pltpu.CompilerParams(vmem_limit_bytes=60 << 20),
        in_specs=[SMEM, VMEM, IN_HBM, ANY] + ([IN_HBM] + [ANY] * (n_y - 1)) * 2,
        out_specs=ANY,
        out_shape=jax.ShapeDtypeStruct(field.shape, f32),
        scratch_shapes=[
            pltpu.VMEM(block, f32),
            pltpu.VMEM(turned, f32),
            pltpu.VMEM((n_y, 2) + turned[1:], f32),
            pltpu.VMEM(block, f32),
            pltpu.SemaphoreType.DMA((n_y, 4)),
            pltpu.SemaphoreType.DMA((n_y,)),
        ],
    )(me, sums, field, h, *firsts, *crosses)


def on_device(field, factor_a, factor_b, factor_c):
    n_y, n_x, n_z = (lax.axis_size(a) for a in ("gy", "x", Z))
    depth, rows, cols = field.shape
    sub = depth // n_y
    me_y = lax.axis_index("gy").reshape(1)
    grid = tuple(lax.axis_size(a) for a in PLANES)
    planes = cols // lax.axis_size(PLANES)

    def shifted(value, axis, d):
        n = lax.axis_size(axis)
        return lax.ppermute(value, axis, [(i, (i + d) % n) for i in range(n)])

    def exchanged(pieces, axis):
        return [shifted(p, axis, d) if d else p for d, p in enumerate(pieces)]

    def all_to_all(value, axes):
        value = value.reshape((-1,) + value.shape[-2:])
        return lax.all_to_all(value, axes, 0, 0, tiled=True)

    turned = field.transpose(2, 0, 1)
    v = all_to_all(turned, PLANES).reshape(grid + (planes, depth, rows))

    piece = (cols, sub, rows)
    rows_in = call(y_pack_kernel, [piece] * n_y, me_y, turned)
    rows_in = exchanged(rows_in, "gy")
    c = split_factor(factor_c)
    at = split_factor(factor_a, lax.axis_size("core") * rows)
    b = split_factor(factor_b)
    bv, size_field = call(
        row_kernel,
        [(n_y,) + piece, (8, 128)],
        me_y,
        *rows_in,
        b,
        scratch=[pltpu.VMEM((n_y,) + piece, f32)],
    )

    g = planes_call(first_kernel, v, at, c, (n_y,) + grid + (planes, sub, rows))
    g_rows = all_to_all(g, ("gy",) + PLANES).reshape(n_y, cols, sub, rows)
    h = planes_call(second_kernel, g, at, c, grid + (planes, depth, rows))
    h = all_to_all(h, PLANES)

    *first, size_first = call(term_kernel, [piece] * n_y + [(8, 128)], me_y, bv, g_rows, own=True)
    sums = jnp.stack([size_field, size_first])
    sums = sums + sum(shifted(sums, "gy", d) for d in range(1, n_y))
    first = exchanged(first, "gy")
    cross = call(cross_kernel, [piece] * n_y, me_y, bv, g_rows, b, own=True)
    cross = exchanged(cross, "gy")
    sums = sums + shifted(sums, "core", 1)
    sums = sums + sum(shifted(sums, "x", d) for d in range(1, n_x))
    sums = sums + sum(shifted(sums, Z, d) for d in range(1, n_z))
    return last_step(me_y, sums, field, h, first, cross)


def solution(mesh):
    finer = Mesh(
        mesh.devices.reshape(4, 2, mesh.shape["gy"], 2, 4), GX + ("gy",) + GZ
    )
    spec = P(GZ, GX, "gy")
    return jax.shard_map(
        on_device, mesh=finer, in_specs=(spec, P(), P(), P()), out_specs=spec, check_vma=False
    )
```

profile of v0, /device:TPU:32, one launch (start us, length us, event | category | flops | bytes accessed | tf_op | source)
XLA Modules:
  0.0 269.1 jit_solution(1165715255041882083)
XLA Ops:
  0.0 3.0 %copy.5 = f32[32,128,128]{1,0,2:T(8,128)} copy(f32[32,128,128]{2,1,0:T(8,128)} %v_ref.1) | data formatting | bytes 4194304 | tf_op args[0]
  3.0 11.7 %all-to-all-start = ((f32[128,32,128]{2,1,0:T(8,128)}), f32[128,32,128]{2,1,0:T(8,128)S(1)}, u32[]{:S(2)}, u32[]{:S(2)}) async-start(f32[128,32,128]{2,1,0:T(8,128)} %bitcast.1.v_ref), calls=%async_computation | async-start | bytes 4194304 | tf_op jit(solution)/shard_map/all_to_all | solution.py:282
  15.5 2.2 copy-done
  17.7 3.0 %shard_map.49.at_ref = bf16[4,2,1024,256]{3,2,1,0:T(8,128)(2,1)} custom-call(f32[1024,1024]{1,0:T(8,128)S(1)} %copy-done), custom_call_target="tpu_custom_call" | custom-call | tf_op jit(solution)/shard_map/pallas_call | solution.py:50
  20.8 43.7 %all-to-all-done = f32[128,32,128]{2,1,0:T(8,128)S(1)} async-done(((f32[128,32,128]{2,1,0:T(8,128)}), f32[128,32,128]{2,1,0:T(8,128)S(1)}, u32[]{:S(2)}, u32[]{:S(2)}) %all-to-all-start) | async-done | bytes 2097184 | tf_op jit(solution)/shard_map/all_to_all | solution.py:282
  65.8 8.4 %shard_map.51.g_ref = f32[4,2,4,2,4,2,8,128]{7,6,5,4,3,2,1,0:T(8,128)} custom-call(f32[2,4,2,4,2,32,128]{6,5,4,3,2,1,0:T(8,128)} %bitcast.16, bf16[4,2,1024,256]{3,2,1,0:T(8,128)(2,1)} %shard_map.49.at_ref, bf16[2,256,256]{2,1,0:T(8,128)(2,1)} %copy-done.1), custom_call_target="tpu_custom_call" | custom-call | tf_op jit(solution)/shard_map/pallas_call | solution.py:155
  74.2 9.9 %all-to-all-start.1 = ((f32[512,8,128]{2,1,0:T(8,128)}), f32[512,8,128]{2,1,0:T(8,128)S(1)}, u32[]{:S(2)}, u32[]{:S(2)}) async-start(f32[512,8,128]{2,1,0:T(8,128)} %bitcast.14), calls=%async_computation.1 | async-start | bytes 4194304 | tf_op jit(solution)/shard_map/all_to_all | solution.py:282
  84.0 8.4 %shard_map.53 = f32[2,4,2,4,2,32,128]{6,5,4,3,2,1,0:T(8,128)} custom-call(f32[4,2,4,2,4,2,8,128]{7,6,5,4,3,2,1,0:T(8,128)} %shard_map.51.g_ref, bf16[4,2,1024,256]{3,2,1,0:T(8,128)(2,1)} %shard_map.49.at_ref, bf16[2,256,256]{2,1,0:T(8,128)(2,1)} %copy-done.1), custom_call_target="tpu_custom_call" | custom-call | tf_op jit(solution)/shard_map/pallas_call | solution.py:155
  92.4 43.9 %all-to-all-done.1 = f32[512,8,128]{2,1,0:T(8,128)S(1)} async-done(((f32[512,8,128]{2,1,0:T(8,128)}), f32[512,8,128]{2,1,0:T(8,128)S(1)}, u32[]{:S(2)}, u32[]{:S(2)}) %all-to-all-start.1) | async-done | bytes 2097184 | tf_op jit(solution)/shard_map/all_to_all | solution.py:282
  136.3 6.7 %all-to-all-start.2 = ((f32[128,32,128]{2,1,0:T(8,128)}), f32[128,32,128]{2,1,0:T(8,128)}, u32[]{:S(2)}, u32[]{:S(2)}) async-start(f32[128,32,128]{2,1,0:T(8,128)} %bitcast.15), calls=%async_computation.2 | async-start | bytes 4194304 | tf_op jit(solution)/shard_map/all_to_all | solution.py:282
  143.0 1.9 shard_map.46
  145.6 1.9 collective-permute-start.1
  150.0 21.5 %collective-permute-done.refs_1_ = f32[128,8,128]{2,1,0:T(8,128)S(1)} collective-permute-done((f32[128,8,128]{2,1,0:T(8,128)S(1)}, f32[128,8,128]{2,1,0:T(8,128)S(1)}, u32[]{:S(2)}, u32[]{:S(2)}) %collective-permute-start) | collective-permute-done | bytes 524320 | tf_op jit(solution)/shard_map/ppermute | solution.py:275
  172.1 2.2 shard_map.48
  174.3 3.3 %shard_map.54 = (f32[128,8,128]{2,1,0:T(8,128)}, f32[128,8,128]{2,1,0:T(8,128)S(1)}, f32[128,8,128]{2,1,0:T(8,128)}, f32[128,8,128]{2,1,0:T(8,128)}) custom-call(s32[1]{0:T(128)} %bitcast.me_ref, f32[4,128,8,128]{3,2,1,0:T(8,128)S(1)} %get-tuple-element.25.bv_ref, f32[4,128,8,128]{3,2,1,0:T(8,128)S(1)} %bitcast.8, ...), custom_call_target="tpu_custom_call" | custom-call | tf_op jit(solution)/shard_map/pallas_call | solution.py:63
  179.3 2.8 %collective-permute-start.5 = (f32[2,8,128]{2,1,0:T(8,128)S(1)}, f32[2,8,128]{2,1,0:T(8,128)S(1)}, u32[]{:S(2)}, u32[]{:S(2)}) collective-permute-start(f32[2,8,128]{2,1,0:T(8,128)S(1)} %pad_maximum_fusion), channel_id=1, source_target_pairs={{0,24},{8,0},{16,8},{24,16},{1,25},{9,1},{17,9},{25,17},{2,26},{10... | collective-permute-start | bytes 24584 | tf_op jit(solution)/shard_map/ppermute | solution.py:275
  182.9 1.4 collective-permute-start.3
  184.3 10.6 %collective-permute-done.4 = f32[2,8,128]{2,1,0:T(8,128)S(1)} collective-permute-done((f32[2,8,128]{2,1,0:T(8,128)S(1)}, f32[2,8,128]{2,1,0:T(8,128)S(1)}, u32[]{:S(2)}, u32[]{:S(2)}) %collective-permute-start.4) | collective-permute-done | bytes 8224 | tf_op jit(solution)/shard_map/ppermute | solution.py:275
  196.2 2.7 %collective-permute-start.9 = (f32[2,8,128]{2,1,0:T(8,128)S(1)}, f32[2,8,128]{2,1,0:T(8,128)S(1)}, u32[]{:S(2)}, u32[]{:S(2)}) collective-permute-start(f32[2,8,128]{2,1,0:T(8,128)S(1)} %add.45), channel_id=1, source_target_pairs={{0,3},{1,0},{2,1},{3,2},{4,7},{5,4},{6,5},{7,6},{8,11},{9,8},{10,9... | collective-permute-start | bytes 24584 | tf_op jit(solution)/shard_map/ppermute | solution.py:275
  200.6 3.4 %collective-permute-done.8 = f32[2,8,128]{2,1,0:T(8,128)S(1)} collective-permute-done((f32[2,8,128]{2,1,0:T(8,128)S(1)}, f32[2,8,128]{2,1,0:T(8,128)S(1)}, u32[]{:S(2)}, u32[]{:S(2)}) %collective-permute-start.8) | collective-permute-done | bytes 8224 | tf_op jit(solution)/shard_map/ppermute | solution.py:275
  205.1 3.7 %collective-permute-start.15 = (f32[2,8,128]{2,1,0:T(8,128)S(1)}, f32[2,8,128]{2,1,0:T(8,128)S(1)}, u32[]{:S(2)}, u32[]{:S(2)}) collective-permute-start(f32[2,8,128]{2,1,0:T(8,128)S(1)} %add_add_fusion.1), channel_id=1, source_target_pairs={{0,192},{4,196},{64,0},{68,4},{128,64},{132,68},{192,128},{196,132... | collective-permute-start | bytes 24584 | tf_op jit(solution)/shard_map/ppermute | solution.py:275
  208.9 2.3 collective-permute-start.14
  211.2 2.8 %collective-permute-start.13 = (f32[2,8,128]{2,1,0:T(8,128)S(1)}, f32[2,8,128]{2,1,0:T(8,128)S(1)}, u32[]{:S(2)}, u32[]{:S(2)}) collective-permute-start(f32[2,8,128]{2,1,0:T(8,128)S(1)} %add_add_fusion.1), channel_id=1, source_target_pairs={{0,128},{4,132},{64,192},{68,196},{128,0},{132,4},{192,64},{196,68... | collective-permute-start | bytes 24584 | tf_op jit(solution)/shard_map/ppermute | solution.py:275
  213.9 2.2 collective-permute-start.12
  216.2 2.4 collective-permute-start.11
  222.6 2.1 collective-permute-start.18
  226.1 9.6 %collective-permute-done.21.refs_6_ = f32[128,8,128]{2,1,0:T(8,128)S(1)} collective-permute-done((f32[128,8,128]{2,1,0:T(8,128)}, f32[128,8,128]{2,1,0:T(8,128)S(1)}, u32[]{:S(2)}, u32[]{:S(2)}) %collective-permute-start.21) | collective-permute-done | bytes 524320 | tf_op jit(solution)/shard_map/ppermute | solution.py:275
  235.7 9.1 %collective-permute-done.22.refs_7_ = f32[128,8,128]{2,1,0:T(8,128)S(1)} collective-permute-done((f32[128,8,128]{2,1,0:T(8,128)}, f32[128,8,128]{2,1,0:T(8,128)S(1)}, u32[]{:S(2)}, u32[]{:S(2)}) %collective-permute-start.22) | collective-permute-done | bytes 524320 | tf_op jit(solution)/shard_map/ppermute | solution.py:275
  244.8 2.0 collective-permute-done.17.refs_1_
  246.8 6.9 %collective-permute-done.18.refs_2_ = f32[128,8,128]{2,1,0:T(8,128)S(1)} collective-permute-done((f32[128,8,128]{2,1,0:T(8,128)}, f32[128,8,128]{2,1,0:T(8,128)S(1)}, u32[]{:S(2)}, u32[]{:S(2)}) %collective-permute-start.18) | collective-permute-done | bytes 524320 | tf_op jit(solution)/shard_map/ppermute | solution.py:275
  253.7 9.3 %collective-permute-done.19.refs_3_ = f32[128,8,128]{2,1,0:T(8,128)} collective-permute-done((f32[128,8,128]{2,1,0:T(8,128)S(1)}, f32[128,8,128]{2,1,0:T(8,128)}, u32[]{:S(2)}, u32[]{:S(2)}) %collective-permute-start.19) | collective-permute-done | bytes 524320 | tf_op jit(solution)/shard_map/ppermute | solution.py:275
  263.0 5.9 %shard_map.55 = f32[32,128,128]{2,1,0:T(8,128)} custom-call(s32[1]{0:T(128)} %bitcast.me_ref, f32[2,8,128]{2,1,0:T(8,128)} %add_add_fusion.sum_ref, f32[32,128,128]{2,1,0:T(8,128)} %v_ref.1, f32[128,32,128]{2,1,0:T(8,128)} %all-to-all-done.2.h_ref, f32[128,8,128]{2,1,0:T(8,128)} %get-tuple-element.27.refs_0_, f32[128,8,128]{2,1,0:T(8,128)} %copy-done.8, ...), custom_call_target="tpu_custom_call" | custom-call | tf_op jit(solution)/shard_map/pallas_call | solution.py:248
  (56 shorter events, 17.8 us)
Async XLA Ops:
  3.0 11.7 %copy-start.3 = (f32[256,256]{1,0:T(8,128)S(1)}, f32[256,256]{1,0:T(8,128)}, u32[]{:S(2)}) copy-start(f32[256,256]{1,0:T(8,128)} %x_ref.5) | copy-start | bytes 786436
  3.0 61.4 %all-to-all-start = ((f32[128,32,128]{2,1,0:T(8,128)}), f32[128,32,128]{2,1,0:T(8,128)S(1)}, u32[]{:S(2)}, u32[]{:S(2)}) async-start(f32[128,32,128]{2,1,0:T(8,128)} %bitcast.1.v_ref), calls=%async_computation | async-start | bytes 4194304 | tf_op jit(solution)/shard_map/all_to_all | solution.py:282
  74.2 62.1 %all-to-all-start.1 = ((f32[512,8,128]{2,1,0:T(8,128)}), f32[512,8,128]{2,1,0:T(8,128)S(1)}, u32[]{:S(2)}, u32[]{:S(2)}) async-start(f32[512,8,128]{2,1,0:T(8,128)} %bitcast.14), calls=%async_computation.1 | async-start | bytes 4194304 | tf_op jit(solution)/shard_map/all_to_all | solution.py:282
  136.3 89.8 %all-to-all-start.2 = ((f32[128,32,128]{2,1,0:T(8,128)}), f32[128,32,128]{2,1,0:T(8,128)}, u32[]{:S(2)}, u32[]{:S(2)}) async-start(f32[128,32,128]{2,1,0:T(8,128)} %bitcast.15), calls=%async_computation.2 | async-start | bytes 4194304 | tf_op jit(solution)/shard_map/all_to_all | solution.py:282
  144.9 26.6 %collective-permute-start = (f32[128,8,128]{2,1,0:T(8,128)S(1)}, f32[128,8,128]{2,1,0:T(8,128)S(1)}, u32[]{:S(2)}, u32[]{:S(2)}) collective-permute-start(f32[128,8,128]{2,1,0:T(8,128)S(1)} %get-tuple-element.21), channel_id=1, source_target_pairs={{0,8},{8,16},{16,24},{24,0},{1,9},{9,17},{17,25},{25,1},{2,10},{10... | collective-permute-start | bytes 1572872 | tf_op jit(solution)/shard_map/ppermute | solution.py:275
  145.6 25.9 %collective-permute-start.1 = (f32[128,8,128]{2,1,0:T(8,128)S(1)}, f32[128,8,128]{2,1,0:T(8,128)S(1)}, u32[]{:S(2)}, u32[]{:S(2)}) collective-permute-start(f32[128,8,128]{2,1,0:T(8,128)S(1)} %get-tuple-element.22), channel_id=1, source_target_pairs={{0,16},{8,24},{16,0},{24,8},{1,17},{9,25},{17,1},{25,9},{2,18},{10... | collective-permute-start | bytes 1572872 | tf_op jit(solution)/shard_map/ppermute | solution.py:275
  147.6 24.6 %collective-permute-start.2 = (f32[128,8,128]{2,1,0:T(8,128)S(1)}, f32[128,8,128]{2,1,0:T(8,128)S(1)}, u32[]{:S(2)}, u32[]{:S(2)}) collective-permute-start(f32[128,8,128]{2,1,0:T(8,128)S(1)} %get-tuple-element.23), channel_id=1, source_target_pairs={{0,24},{8,0},{16,8},{24,16},{1,25},{9,1},{17,9},{25,17},{2,26},{10... | collective-permute-start | bytes 1572872 | tf_op jit(solution)/shard_map/ppermute | solution.py:275
  178.9 45.9 %collective-permute-start.20 = (f32[128,8,128]{2,1,0:T(8,128)S(1)}, f32[128,8,128]{2,1,0:T(8,128)S(1)}, u32[]{:S(2)}, u32[]{:S(2)}) collective-permute-start(f32[128,8,128]{2,1,0:T(8,128)S(1)} %get-tuple-element.32), channel_id=1, source_target_pairs={{0,8},{8,16},{16,24},{24,0},{1,9},{9,17},{17,25},{25,1},{2,10},{10... | collective-permute-start | bytes 1572872 | tf_op jit(solution)/shard_map/ppermute | solution.py:275
  179.3 5.0 %collective-permute-start.5 = (f32[2,8,128]{2,1,0:T(8,128)S(1)}, f32[2,8,128]{2,1,0:T(8,128)S(1)}, u32[]{:S(2)}, u32[]{:S(2)}) collective-permute-start(f32[2,8,128]{2,1,0:T(8,128)S(1)} %pad_maximum_fusion), channel_id=1, source_target_pairs={{0,24},{8,0},{16,8},{24,16},{1,25},{9,1},{17,9},{25,17},{2,26},{10... | collective-permute-start | bytes 24584 | tf_op jit(solution)/shard_map/ppermute | solution.py:275
  182.1 12.8 %collective-permute-start.4 = (f32[2,8,128]{2,1,0:T(8,128)S(1)}, f32[2,8,128]{2,1,0:T(8,128)S(1)}, u32[]{:S(2)}, u32[]{:S(2)}) collective-permute-start(f32[2,8,128]{2,1,0:T(8,128)S(1)} %pad_maximum_fusion), channel_id=1, source_target_pairs={{0,16},{8,24},{16,0},{24,8},{1,17},{9,25},{17,1},{25,9},{2,18},{10... | collective-permute-start | bytes 24584 | tf_op jit(solution)/shard_map/ppermute | solution.py:275
  182.9 12.0 %collective-permute-start.3 = (f32[2,8,128]{2,1,0:T(8,128)S(1)}, f32[2,8,128]{2,1,0:T(8,128)S(1)}, u32[]{:S(2)}, u32[]{:S(2)}) collective-permute-start(f32[2,8,128]{2,1,0:T(8,128)S(1)} %pad_maximum_fusion), channel_id=1, source_target_pairs={{0,8},{8,16},{16,24},{24,0},{1,9},{9,17},{17,25},{25,1},{2,10},{10... | collective-permute-start | bytes 24584 | tf_op jit(solution)/shard_map/ppermute | solution.py:275
  194.9 1.3 collective-permute-start.6
  196.2 4.4 %collective-permute-start.9 = (f32[2,8,128]{2,1,0:T(8,128)S(1)}, f32[2,8,128]{2,1,0:T(8,128)S(1)}, u32[]{:S(2)}, u32[]{:S(2)}) collective-permute-start(f32[2,8,128]{2,1,0:T(8,128)S(1)} %add.45), channel_id=1, source_target_pairs={{0,3},{1,0},{2,1},{3,2},{4,7},{5,4},{6,5},{7,6},{8,11},{9,8},{10,9... | collective-permute-start | bytes 24584 | tf_op jit(solution)/shard_map/ppermute | solution.py:275
  198.9 5.2 %collective-permute-start.8 = (f32[2,8,128]{2,1,0:T(8,128)S(1)}, f32[2,8,128]{2,1,0:T(8,128)S(1)}, u32[]{:S(2)}, u32[]{:S(2)}) collective-permute-start(f32[2,8,128]{2,1,0:T(8,128)S(1)} %add.45), channel_id=1, source_target_pairs={{0,2},{1,3},{2,0},{3,1},{4,6},{5,7},{6,4},{7,5},{8,10},{9,11},{10,... | collective-permute-start | bytes 24584 | tf_op jit(solution)/shard_map/ppermute | solution.py:275
  199.7 4.9 %collective-permute-start.7 = (f32[2,8,128]{2,1,0:T(8,128)S(1)}, f32[2,8,128]{2,1,0:T(8,128)S(1)}, u32[]{:S(2)}, u32[]{:S(2)}) collective-permute-start(f32[2,8,128]{2,1,0:T(8,128)S(1)} %add.45), channel_id=1, source_target_pairs={{0,1},{1,2},{2,3},{3,0},{4,5},{5,6},{6,7},{7,4},{8,9},{9,10},{10,1... | collective-permute-start | bytes 24584 | tf_op jit(solution)/shard_map/ppermute | solution.py:275
  204.6 9.3 %collective-permute-start.16 = (f32[2,8,128]{2,1,0:T(8,128)S(1)}, f32[2,8,128]{2,1,0:T(8,128)S(1)}, u32[]{:S(2)}, u32[]{:S(2)}) collective-permute-start(f32[2,8,128]{2,1,0:T(8,128)S(1)} %add_add_fusion.1), channel_id=1, source_target_pairs={{0,196},{4,0},{64,4},{68,64},{128,68},{132,128},{192,132},{196,192... | collective-permute-start | bytes 24584 | tf_op jit(solution)/shard_map/ppermute | solution.py:275
  205.1 11.0 %collective-permute-start.15 = (f32[2,8,128]{2,1,0:T(8,128)S(1)}, f32[2,8,128]{2,1,0:T(8,128)S(1)}, u32[]{:S(2)}, u32[]{:S(2)}) collective-permute-start(f32[2,8,128]{2,1,0:T(8,128)S(1)} %add_add_fusion.1), channel_id=1, source_target_pairs={{0,192},{4,196},{64,0},{68,4},{128,64},{132,68},{192,128},{196,132... | collective-permute-start | bytes 24584 | tf_op jit(solution)/shard_map/ppermute | solution.py:275
  208.9 9.7 %collective-permute-start.14 = (f32[2,8,128]{2,1,0:T(8,128)S(1)}, f32[2,8,128]{2,1,0:T(8,128)S(1)}, u32[]{:S(2)}, u32[]{:S(2)}) collective-permute-start(f32[2,8,128]{2,1,0:T(8,128)S(1)} %add_add_fusion.1), channel_id=1, source_target_pairs={{0,132},{4,192},{64,196},{68,0},{128,4},{132,64},{192,68},{196,128... | collective-permute-start | bytes 24584 | tf_op jit(solution)/shard_map/ppermute | solution.py:275
  211.2 8.0 %collective-permute-start.13 = (f32[2,8,128]{2,1,0:T(8,128)S(1)}, f32[2,8,128]{2,1,0:T(8,128)S(1)}, u32[]{:S(2)}, u32[]{:S(2)}) collective-permute-start(f32[2,8,128]{2,1,0:T(8,128)S(1)} %add_add_fusion.1), channel_id=1, source_target_pairs={{0,128},{4,132},{64,192},{68,196},{128,0},{132,4},{192,64},{196,68... | collective-permute-start | bytes 24584 | tf_op jit(solution)/shard_map/ppermute | solution.py:275
  213.9 6.7 %collective-permute-start.12 = (f32[2,8,128]{2,1,0:T(8,128)S(1)}, f32[2,8,128]{2,1,0:T(8,128)S(1)}, u32[]{:S(2)}, u32[]{:S(2)}) collective-permute-start(f32[2,8,128]{2,1,0:T(8,128)S(1)} %add_add_fusion.1), channel_id=1, source_target_pairs={{0,68},{4,128},{64,132},{68,192},{128,196},{132,0},{192,4},{196,64... | collective-permute-start | bytes 24584 | tf_op jit(solution)/shard_map/ppermute | solution.py:275
  216.2 5.8 %collective-permute-start.11 = (f32[2,8,128]{2,1,0:T(8,128)S(1)}, f32[2,8,128]{2,1,0:T(8,128)S(1)}, u32[]{:S(2)}, u32[]{:S(2)}) collective-permute-start(f32[2,8,128]{2,1,0:T(8,128)S(1)} %add_add_fusion.1), channel_id=1, source_target_pairs={{0,64},{4,68},{64,128},{68,132},{128,192},{132,196},{192,0},{196,4... | collective-permute-start | bytes 24584 | tf_op jit(solution)/shard_map/ppermute | solution.py:275
  218.6 4.0 %collective-permute-start.10 = (f32[2,8,128]{2,1,0:T(8,128)S(1)}, f32[2,8,128]{2,1,0:T(8,128)S(1)}, u32[]{:S(2)}, u32[]{:S(2)}) collective-permute-start(f32[2,8,128]{2,1,0:T(8,128)S(1)} %add_add_fusion.1), channel_id=1, source_target_pairs={{0,4},{4,64},{64,68},{68,128},{128,132},{132,192},{192,196},{196,0... | collective-permute-start | bytes 24584 | tf_op jit(solution)/shard_map/ppermute | solution.py:275
  219.2 16.5 %collective-permute-start.21 = (f32[128,8,128]{2,1,0:T(8,128)}, f32[128,8,128]{2,1,0:T(8,128)S(1)}, u32[]{:S(2)}, u32[]{:S(2)}) collective-permute-start(f32[128,8,128]{2,1,0:T(8,128)} %get-tuple-element.33), channel_id=1, source_target_pairs={{0,16},{8,24},{16,0},{24,8},{1,17},{9,25},{17,1},{25,9},{2,18},{10... | collective-permute-start | bytes 1572872 | tf_op jit(solution)/shard_map/ppermute | solution.py:275
  220.6 24.2 %collective-permute-start.22 = (f32[128,8,128]{2,1,0:T(8,128)}, f32[128,8,128]{2,1,0:T(8,128)S(1)}, u32[]{:S(2)}, u32[]{:S(2)}) collective-permute-start(f32[128,8,128]{2,1,0:T(8,128)} %get-tuple-element.34), channel_id=1, source_target_pairs={{0,24},{8,0},{16,8},{24,16},{1,25},{9,1},{17,9},{25,17},{2,26},{10... | collective-permute-start | bytes 1572872 | tf_op jit(solution)/shard_map/ppermute | solution.py:275
  221.9 24.9 %collective-permute-start.17 = (f32[128,8,128]{2,1,0:T(8,128)}, f32[128,8,128]{2,1,0:T(8,128)S(1)}, u32[]{:S(2)}, u32[]{:S(2)}) collective-permute-start(f32[128,8,128]{2,1,0:T(8,128)} %get-tuple-element.28), channel_id=1, source_target_pairs={{0,8},{8,16},{16,24},{24,0},{1,9},{9,17},{17,25},{25,1},{2,10},{10... | collective-permute-start | bytes 1572872 | tf_op jit(solution)/shard_map/ppermute | solution.py:275
  222.6 31.1 %collective-permute-start.18 = (f32[128,8,128]{2,1,0:T(8,128)}, f32[128,8,128]{2,1,0:T(8,128)S(1)}, u32[]{:S(2)}, u32[]{:S(2)}) collective-permute-start(f32[128,8,128]{2,1,0:T(8,128)} %get-tuple-element.29), channel_id=1, source_target_pairs={{0,16},{8,24},{16,0},{24,8},{1,17},{9,25},{17,1},{25,9},{2,18},{10... | collective-permute-start | bytes 1572872 | tf_op jit(solution)/shard_map/ppermute | solution.py:275
  224.8 38.3 %copy-start.5 = (f32[128,8,128]{2,1,0:T(8,128)}, f32[128,8,128]{2,1,0:T(8,128)S(1)}, u32[]{:S(2)}) copy-start(f32[128,8,128]{2,1,0:T(8,128)S(1)} %collective-permute-done.20.refs_5_) | copy-start | bytes 1572868
  224.8 38.3 %collective-permute-start.19 = (f32[128,8,128]{2,1,0:T(8,128)S(1)}, f32[128,8,128]{2,1,0:T(8,128)}, u32[]{:S(2)}, u32[]{:S(2)}) collective-permute-start(f32[128,8,128]{2,1,0:T(8,128)S(1)} %get-tuple-element.30), channel_id=1, source_target_pairs={{0,24},{8,0},{16,8},{24,16},{1,25},{9,1},{17,9},{25,17},{2,26},{10... | collective-permute-start | bytes 1572872 | tf_op jit(solution)/shard_map/ppermute | solution.py:275
  235.7 27.3 %copy-start.6 = (f32[128,8,128]{2,1,0:T(8,128)}, f32[128,8,128]{2,1,0:T(8,128)S(1)}, u32[]{:S(2)}) copy-start(f32[128,8,128]{2,1,0:T(8,128)S(1)} %collective-permute-done.21.refs_6_) | copy-start | bytes 1572868
  244.8 18.2 %copy-start.7 = (f32[128,8,128]{2,1,0:T(8,128)}, f32[128,8,128]{2,1,0:T(8,128)S(1)}, u32[]{:S(2)}) copy-start(f32[128,8,128]{2,1,0:T(8,128)S(1)} %collective-permute-done.22.refs_7_) | copy-start | bytes 1572868
  246.8 16.2 %copy-start.8 = (f32[128,8,128]{2,1,0:T(8,128)}, f32[128,8,128]{2,1,0:T(8,128)S(1)}, u32[]{:S(2)}) copy-start(f32[128,8,128]{2,1,0:T(8,128)S(1)} %collective-permute-done.17.refs_1_) | copy-start | bytes 1572868
  253.7 9.3 %copy-start.9 = (f32[128,8,128]{2,1,0:T(8,128)}, f32[128,8,128]{2,1,0:T(8,128)S(1)}, u32[]{:S(2)}) copy-start(f32[128,8,128]{2,1,0:T(8,128)S(1)} %collective-permute-done.18.refs_2_) | copy-start | bytes 1572868
  (4 other events, 5.5 us)
where the time goes:
time: 271 us; the launch traced here: 269 us
  waiting for transfers between devices  164 us (61%)
  starting transfers between devices  60.7 us (22%)
  Pallas kernels  34.5 us (13%)
  local copies, waits for them, and re-layouts  8.55 us (3%)
    all_to_all x3, waiting for transfers between devices, all_to_all(): return lax.all_to_all(value, axes, 0, 0, tiled=True)  87.5 us
    ppermute x23, waiting for transfers between devices, shifted(): return lax.ppermute(value, axis, [(i, (i + d) % n) for i in range(n)])  76.9 us
    ppermute x23, starting transfers between devices, shifted(): return lax.ppermute(value, axis, [(i, (i + d) % n) for i in range(n)])  32.4 us
    all_to_all x3, starting transfers between devices, all_to_all(): return lax.all_to_all(value, axes, 0, 0, tiled=True)  28.3 us
    pallas_call x2, Pallas kernels, planes_call(): pl.pallas_call(kernel, compiler_params=pltpu.CompilerParams(vmem_limit_by...  16.7 us
    pallas_call x4, Pallas kernels, call(): pl.pallas_call(kernel, compiler_params=LIMIT, out_shape=[HBM(s, f32) if o...  8.62 us
    unnamed x21, local copies, waits for them, and re-layouts  8.55 us
    pallas_call x1, Pallas kernels, last_step(): pl.pallas_call(last_kernel, compiler_params=pltpu.CompilerParams(vmem_lim...  5.88 us
  transfers between devices with their start and end apart: 26, of which 15 were waited for; matrix products, arithmetic and copies ran while one was open for 0% of the time, Pallas kernels for 8%

commit v1 on v0

--- a/solution.py
+++ b/solution.py
@@ -21,6 +21,10 @@
 VMEM, SMEM, ANY, IN_HBM = (
     pl.BlockSpec(memory_space=s) for s in (pltpu.VMEM, pltpu.SMEM, pl.ANY, HBM)
 )
+
+
+def far(x):
+    return pltpu.with_memory_space_constraint(x, HBM)
 
 
 def halves(x):
@@ -154,13 +158,13 @@
     index = lambda i: tuple(i if d == zh else 0 for d in range(len(shape)))
     return pl.pallas_call(
         kernel,
-        compiler_params=pltpu.CompilerParams(vmem_limit_bytes=61 << 20),
+        compiler_params=LIMIT,
         grid=(n_zh,),
         in_specs=[whole(value), pl.BlockSpec((1,) + at.shape[1:], lambda i: (i, 0, 0, 0)), whole(c)],
         out_specs=pl.BlockSpec(shape[:zh] + (1,) + shape[zh + 1 :], index),
         out_shape=HBM(shape, f32),
         scratch_shapes=[pltpu.VMEM((2, shape[-3] * m, n), bf16)],
-    )(value, at, c)
+    )(value, far(at), c)
 
 
 def y_pack_kernel(me_ref, v_ref, *o_refs):
@@ -247,7 +251,7 @@
     block, turned = (n_y, sub, rows, cols), (n_y, cols, sub, rows)
     return pl.pallas_call(
         last_kernel,
-        compiler_params=pltpu.CompilerParams(vmem_limit_bytes=60 << 20),
+        compiler_params=LIMIT,
         in_specs=[SMEM, VMEM, IN_HBM, ANY] + ([IN_HBM] + [ANY] * (n_y - 1)) * 2,
         out_specs=ANY,
         out_shape=jax.ShapeDtypeStruct(field.shape, f32),
@@ -259,7 +263,7 @@
             pltpu.SemaphoreType.DMA((n_y, 4)),
             pltpu.SemaphoreType.DMA((n_y,)),
         ],
-    )(me, sums, field, h, *firsts, *crosses)
+    )(me, sums, far(field), far(h), far(firsts[0]), *firsts[1:], far(crosses[0]), *crosses[1:])
 
 
 def on_device(field, factor_a, factor_b, factor_c):

time: 271 us -> 268 us (0.989)
  Pallas kernels: 34.5 us -> 31.7 us
    pallas_call x3, Pallas kernels: 22.6 us -> 19.6 us  [the longest x2 15.3 us: planes_call(): pl.pallas_call(kernel, compiler_params=LIMIT, grid=(n_zh,), in_specs=[who...]
    unnamed x21 -> x9, local copies, waits for them, and re-layouts: 8.55 us -> 6.84 us
  transfers between devices with their start and end apart: 26 -> 26, of which waited for: 15 -> 15; matrix products, arithmetic and copies ran while one was open for 0% -> 0% of each run, Pallas kernels for 8% -> 7%
where the time goes in v1:
time: 268 us; the launch traced here: 266 us
  waiting for transfers between devices  166 us (62%)
  starting transfers between devices  60.6 us (23%)
  Pallas kernels  31.7 us (12%)
  local copies, waits for them, and re-layouts  6.84 us (3%)
    all_to_all x3, waiting for transfers between devices, all_to_all(): return lax.all_to_all(value, axes, 0, 0, tiled=True)  87.4 us
    ppermute x23, waiting for transfers between devices, shifted(): return lax.ppermute(value, axis, [(i, (i + d) % n) for i in range(n)])  78.7 us
    ppermute x23, starting transfers between devices, shifted(): return lax.ppermute(value, axis, [(i, (i + d) % n) for i in range(n)])  32.3 us
    all_to_all x3, starting transfers between devices, all_to_all(): return lax.all_to_all(value, axes, 0, 0, tiled=True)  28.3 us
    pallas_call x2, Pallas kernels, planes_call(): pl.pallas_call(kernel, compiler_params=LIMIT, grid=(n_zh,), in_specs=[who...  15.3 us
    pallas_call x4, Pallas kernels, call(): pl.pallas_call(kernel, compiler_params=LIMIT, out_shape=[HBM(s, f32) if o...  8.97 us
    unnamed x9, local copies, waits for them, and re-layouts  6.84 us
  transfers between devices with their start and end apart: 26, of which 15 were waited for; matrix products, arithmetic and copies ran while one was open for 0% of the time, Pallas kernels for 7%

profile of v1, /device:TPU:32, one launch (start us, length us, event | category | flops | bytes accessed | tf_op | source)
XLA Modules:
  0.0 265.6 jit_solution(3077500680060320427)
XLA Ops:
  0.0 3.0 %copy.5 = f32[32,128,128]{1,0,2:T(8,128)} copy(f32[32,128,128]{2,1,0:T(8,128)} %v_ref.1) | data formatting | bytes 4194304 | tf_op args[0]
  3.0 11.7 %all-to-all-start = ((f32[128,32,128]{2,1,0:T(8,128)}), f32[128,32,128]{2,1,0:T(8,128)S(1)}, u32[]{:S(2)}, u32[]{:S(2)}) async-start(f32[128,32,128]{2,1,0:T(8,128)} %bitcast.1.v_ref), calls=%async_computation | async-start | bytes 4194304 | tf_op jit(solution)/shard_map/all_to_all | solution.py:286
  14.8 2.2 copy-done.1
  17.0 3.0 %shard_map.49.at_ref = bf16[4,2,1024,256]{3,2,1,0:T(8,128)(2,1)} custom-call(f32[1024,1024]{1,0:T(8,128)S(1)} %copy-done.1), custom_call_target="tpu_custom_call" | custom-call | tf_op jit(solution)/shard_map/pallas_call | solution.py:54
  20.0 44.4 %all-to-all-done = f32[128,32,128]{2,1,0:T(8,128)S(1)} async-done(((f32[128,32,128]{2,1,0:T(8,128)}), f32[128,32,128]{2,1,0:T(8,128)S(1)}, u32[]{:S(2)}, u32[]{:S(2)}) %all-to-all-start) | async-done | bytes 2097184 | tf_op jit(solution)/shard_map/all_to_all | solution.py:286
  64.4 7.7 %shard_map.51.g_ref = f32[4,2,4,2,4,2,8,128]{7,6,5,4,3,2,1,0:T(8,128)} custom-call(f32[2,4,2,4,2,32,128]{6,5,4,3,2,1,0:T(8,128)S(1)} %bitcast.11, bf16[4,2,1024,256]{3,2,1,0:T(8,128)(2,1)} %shard_map.49.at_ref, bf16[2,256,256]{2,1,0:T(8,128)(2,1)S(1)} %shard_map.50.c_ref), custom_call_target="tpu_custom_call" | custom-call | tf_op jit(solution)/shard_map/pallas_call | solution.py:159
  72.1 9.9 %all-to-all-start.1 = ((f32[512,8,128]{2,1,0:T(8,128)}), f32[512,8,128]{2,1,0:T(8,128)S(1)}, u32[]{:S(2)}, u32[]{:S(2)}) async-start(f32[512,8,128]{2,1,0:T(8,128)} %bitcast.10), calls=%async_computation.1 | async-start | bytes 4194304 | tf_op jit(solution)/shard_map/all_to_all | solution.py:286
  82.0 1.6 copy-done
  83.6 7.7 %shard_map.53 = f32[2,4,2,4,2,32,128]{6,5,4,3,2,1,0:T(8,128)} custom-call(f32[4,2,4,2,4,2,8,128]{7,6,5,4,3,2,1,0:T(8,128)S(1)} %copy-done, bf16[4,2,1024,256]{3,2,1,0:T(8,128)(2,1)} %shard_map.49.at_ref, bf16[2,256,256]{2,1,0:T(8,128)(2,1)S(1)} %shard_map.50.c_ref), custom_call_target="tpu_custom_call" | custom-call | tf_op jit(solution)/shard_map/pallas_call | solution.py:159
  91.3 43.0 %all-to-all-done.1 = f32[512,8,128]{2,1,0:T(8,128)S(1)} async-done(((f32[512,8,128]{2,1,0:T(8,128)}), f32[512,8,128]{2,1,0:T(8,128)S(1)}, u32[]{:S(2)}, u32[]{:S(2)}) %all-to-all-start.1) | async-done | bytes 2097184 | tf_op jit(solution)/shard_map/all_to_all | solution.py:286
  134.2 6.7 %all-to-all-start.2 = ((f32[128,32,128]{2,1,0:T(8,128)}), f32[128,32,128]{2,1,0:T(8,128)}, u32[]{:S(2)}, u32[]{:S(2)}) async-start(f32[128,32,128]{2,1,0:T(8,128)} %bitcast.16), calls=%async_computation.2 | async-start | bytes 4194304 | tf_op jit(solution)/shard_map/all_to_all | solution.py:286
  141.0 2.0 shard_map.46
  143.6 1.9 collective-permute-start.1
  146.8 22.7 %collective-permute-done.refs_1_ = f32[128,8,128]{2,1,0:T(8,128)S(1)} collective-permute-done((f32[128,8,128]{2,1,0:T(8,128)S(1)}, f32[128,8,128]{2,1,0:T(8,128)S(1)}, u32[]{:S(2)}, u32[]{:S(2)}) %collective-permute-start) | collective-permute-done | bytes 524320 | tf_op jit(solution)/shard_map/ppermute | solution.py:279
  170.2 2.2 shard_map.48
  172.4 3.3 %shard_map.54 = (f32[128,8,128]{2,1,0:T(8,128)}, f32[128,8,128]{2,1,0:T(8,128)S(1)}, f32[128,8,128]{2,1,0:T(8,128)}, f32[128,8,128]{2,1,0:T(8,128)}) custom-call(s32[1]{0:T(128)} %bitcast.me_ref, f32[4,128,8,128]{3,2,1,0:T(8,128)S(1)} %get-tuple-element.25.bv_ref, f32[4,128,8,128]{3,2,1,0:T(8,128)S(1)} %bitcast.8, ...), custom_call_target="tpu_custom_call" | custom-call | tf_op jit(solution)/shard_map/pallas_call | solution.py:67
  177.6 2.8 %collective-permute-start.5 = (f32[2,8,128]{2,1,0:T(8,128)S(1)}, f32[2,8,128]{2,1,0:T(8,128)S(1)}, u32[]{:S(2)}, u32[]{:S(2)}) collective-permute-start(f32[2,8,128]{2,1,0:T(8,128)S(1)} %pad_maximum_fusion), channel_id=1, source_target_pairs={{0,24},{8,0},{16,8},{24,16},{1,25},{9,1},{17,9},{25,17},{2,26},{10... | collective-permute-start | bytes 24584 | tf_op jit(solution)/shard_map/ppermute | solution.py:279
  182.6 10.6 %collective-permute-done.4 = f32[2,8,128]{2,1,0:T(8,128)S(1)} collective-permute-done((f32[2,8,128]{2,1,0:T(8,128)S(1)}, f32[2,8,128]{2,1,0:T(8,128)S(1)}, u32[]{:S(2)}, u32[]{:S(2)}) %collective-permute-start.4) | collective-permute-done | bytes 8224 | tf_op jit(solution)/shard_map/ppermute | solution.py:279
  194.5 2.7 %collective-permute-start.9 = (f32[2,8,128]{2,1,0:T(8,128)S(1)}, f32[2,8,128]{2,1,0:T(8,128)S(1)}, u32[]{:S(2)}, u32[]{:S(2)}) collective-permute-start(f32[2,8,128]{2,1,0:T(8,128)S(1)} %add.45), channel_id=1, source_target_pairs={{0,3},{1,0},{2,1},{3,2},{4,7},{5,4},{6,5},{7,6},{8,11},{9,8},{10,9... | collective-permute-start | bytes 24584 | tf_op jit(solution)/shard_map/ppermute | solution.py:279
  198.9 3.4 %collective-permute-done.8 = f32[2,8,128]{2,1,0:T(8,128)S(1)} collective-permute-done((f32[2,8,128]{2,1,0:T(8,128)S(1)}, f32[2,8,128]{2,1,0:T(8,128)S(1)}, u32[]{:S(2)}, u32[]{:S(2)}) %collective-permute-start.8) | collective-permute-done | bytes 8224 | tf_op jit(solution)/shard_map/ppermute | solution.py:279
  203.4 3.7 %collective-permute-start.15 = (f32[2,8,128]{2,1,0:T(8,128)S(1)}, f32[2,8,128]{2,1,0:T(8,128)S(1)}, u32[]{:S(2)}, u32[]{:S(2)}) collective-permute-start(f32[2,8,128]{2,1,0:T(8,128)S(1)} %add_add_fusion.1), channel_id=1, source_target_pairs={{0,192},{4,196},{64,0},{68,4},{128,64},{132,68},{192,128},{196,132... | collective-permute-start | bytes 24584 | tf_op jit(solution)/shard_map/ppermute | solution.py:279
  207.2 2.3 collective-permute-start.14
  209.4 2.8 %collective-permute-start.13 = (f32[2,8,128]{2,1,0:T(8,128)S(1)}, f32[2,8,128]{2,1,0:T(8,128)S(1)}, u32[]{:S(2)}, u32[]{:S(2)}) collective-permute-start(f32[2,8,128]{2,1,0:T(8,128)S(1)} %add_add_fusion.1), channel_id=1, source_target_pairs={{0,128},{4,132},{64,192},{68,196},{128,0},{132,4},{192,64},{196,68... | collective-permute-start | bytes 24584 | tf_op jit(solution)/shard_map/ppermute | solution.py:279
  212.2 2.2 collective-permute-start.12
  214.5 2.4 collective-permute-start.11
  220.9 2.1 collective-permute-start.18
  223.7 10.2 %collective-permute-done.21.refs_6_ = f32[128,8,128]{2,1,0:T(8,128)S(1)} collective-permute-done((f32[128,8,128]{2,1,0:T(8,128)}, f32[128,8,128]{2,1,0:T(8,128)S(1)}, u32[]{:S(2)}, u32[]{:S(2)}) %collective-permute-start.21) | collective-permute-done | bytes 524320 | tf_op jit(solution)/shard_map/ppermute | solution.py:279
  234.0 9.1 %collective-permute-done.22.refs_7_ = f32[128,8,128]{2,1,0:T(8,128)S(1)} collective-permute-done((f32[128,8,128]{2,1,0:T(8,128)}, f32[128,8,128]{2,1,0:T(8,128)S(1)}, u32[]{:S(2)}, u32[]{:S(2)}) %collective-permute-start.22) | collective-permute-done | bytes 524320 | tf_op jit(solution)/shard_map/ppermute | solution.py:279
  243.1 2.0 collective-permute-done.17.refs_1_
  245.1 6.9 %collective-permute-done.18.refs_2_ = f32[128,8,128]{2,1,0:T(8,128)S(1)} collective-permute-done((f32[128,8,128]{2,1,0:T(8,128)}, f32[128,8,128]{2,1,0:T(8,128)S(1)}, u32[]{:S(2)}, u32[]{:S(2)}) %collective-permute-start.18) | collective-permute-done | bytes 524320 | tf_op jit(solution)/shard_map/ppermute | solution.py:279
  252.0 9.2 %collective-permute-done.19.refs_3_ = f32[128,8,128]{2,1,0:T(8,128)S(1)} collective-permute-done((f32[128,8,128]{2,1,0:T(8,128)}, f32[128,8,128]{2,1,0:T(8,128)S(1)}, u32[]{:S(2)}, u32[]{:S(2)}) %collective-permute-start.19) | collective-permute-done | bytes 524320 | tf_op jit(solution)/shard_map/ppermute | solution.py:279
  261.2 4.2 %shard_map.55 = f32[32,128,128]{2,1,0:T(8,128)} custom-call(s32[1]{0:T(128)} %bitcast.me_ref, f32[2,8,128]{2,1,0:T(8,128)S(1)} %add_add_fusion.sum_ref, f32[32,128,128]{2,1,0:T(8,128)} %v_ref.1, f32[128,32,128]{2,1,0:T(8,128)} %all-to-all-done.2.h_ref, f32[128,8,128]{2,1,0:T(8,128)} %get-tuple-element.27.refs_0_, ...), custom_call_target="tpu_custom_call" | custom-call | tf_op jit(solution)/shard_map/pallas_call | solution.py:252
  (44 shorter events, 15.5 us)
Async XLA Ops:
  3.0 11.7 %copy-start.3 = (f32[256,256]{1,0:T(8,128)S(1)}, f32[256,256]{1,0:T(8,128)}, u32[]{:S(2)}) copy-start(f32[256,256]{1,0:T(8,128)} %x_ref.5) | copy-start | bytes 786436
  3.0 61.4 %all-to-all-start = ((f32[128,32,128]{2,1,0:T(8,128)}), f32[128,32,128]{2,1,0:T(8,128)S(1)}, u32[]{:S(2)}, u32[]{:S(2)}) async-start(f32[128,32,128]{2,1,0:T(8,128)} %bitcast.1.v_ref), calls=%async_computation | async-start | bytes 4194304 | tf_op jit(solution)/shard_map/all_to_all | solution.py:286
  14.8 2.2 copy-start.1
  72.1 62.1 %all-to-all-start.1 = ((f32[512,8,128]{2,1,0:T(8,128)}), f32[512,8,128]{2,1,0:T(8,128)S(1)}, u32[]{:S(2)}, u32[]{:S(2)}) async-start(f32[512,8,128]{2,1,0:T(8,128)} %bitcast.10), calls=%async_computation.1 | async-start | bytes 4194304 | tf_op jit(solution)/shard_map/all_to_all | solution.py:286
  82.0 1.6 copy-start
  134.2 89.5 %all-to-all-start.2 = ((f32[128,32,128]{2,1,0:T(8,128)}), f32[128,32,128]{2,1,0:T(8,128)}, u32[]{:S(2)}, u32[]{:S(2)}) async-start(f32[128,32,128]{2,1,0:T(8,128)} %bitcast.16), calls=%async_computation.2 | async-start | bytes 4194304 | tf_op jit(solution)/shard_map/all_to_all | solution.py:286
  141.0 5.7 %copy-start.2 = (f32[512,512]{1,0:T(8,128)S(1)}, f32[512,512]{1,0:T(8,128)}, u32[]{:S(2)}) copy-start(f32[512,512]{1,0:T(8,128)} %x_ref.3) | copy-start | bytes 3145732
  142.9 26.6 %collective-permute-start = (f32[128,8,128]{2,1,0:T(8,128)S(1)}, f32[128,8,128]{2,1,0:T(8,128)S(1)}, u32[]{:S(2)}, u32[]{:S(2)}) collective-permute-start(f32[128,8,128]{2,1,0:T(8,128)S(1)} %get-tuple-element.21), channel_id=1, source_target_pairs={{0,8},{8,16},{16,24},{24,0},{1,9},{9,17},{17,25},{25,1},{2,10},{10... | collective-permute-start | bytes 1572872 | tf_op jit(solution)/shard_map/ppermute | solution.py:279
  143.6 25.9 %collective-permute-start.1 = (f32[128,8,128]{2,1,0:T(8,128)S(1)}, f32[128,8,128]{2,1,0:T(8,128)S(1)}, u32[]{:S(2)}, u32[]{:S(2)}) collective-permute-start(f32[128,8,128]{2,1,0:T(8,128)S(1)} %get-tuple-element.22), channel_id=1, source_target_pairs={{0,16},{8,24},{16,0},{24,8},{1,17},{9,25},{17,1},{25,9},{2,18},{10... | collective-permute-start | bytes 1572872 | tf_op jit(solution)/shard_map/ppermute | solution.py:279
  145.6 24.6 %collective-permute-start.2 = (f32[128,8,128]{2,1,0:T(8,128)S(1)}, f32[128,8,128]{2,1,0:T(8,128)S(1)}, u32[]{:S(2)}, u32[]{:S(2)}) collective-permute-start(f32[128,8,128]{2,1,0:T(8,128)S(1)} %get-tuple-element.23), channel_id=1, source_target_pairs={{0,24},{8,0},{16,8},{24,16},{1,25},{9,1},{17,9},{25,17},{2,26},{10... | collective-permute-start | bytes 1572872 | tf_op jit(solution)/shard_map/ppermute | solution.py:279
  177.2 45.9 %collective-permute-start.20 = (f32[128,8,128]{2,1,0:T(8,128)S(1)}, f32[128,8,128]{2,1,0:T(8,128)S(1)}, u32[]{:S(2)}, u32[]{:S(2)}) collective-permute-start(f32[128,8,128]{2,1,0:T(8,128)S(1)} %get-tuple-element.32), channel_id=1, source_target_pairs={{0,8},{8,16},{16,24},{24,0},{1,9},{9,17},{17,25},{25,1},{2,10},{10... | collective-permute-start | bytes 1572872 | tf_op jit(solution)/shard_map/ppermute | solution.py:279
  177.6 5.0 %collective-permute-start.5 = (f32[2,8,128]{2,1,0:T(8,128)S(1)}, f32[2,8,128]{2,1,0:T(8,128)S(1)}, u32[]{:S(2)}, u32[]{:S(2)}) collective-permute-start(f32[2,8,128]{2,1,0:T(8,128)S(1)} %pad_maximum_fusion), channel_id=1, source_target_pairs={{0,24},{8,0},{16,8},{24,16},{1,25},{9,1},{17,9},{25,17},{2,26},{10... | collective-permute-start | bytes 24584 | tf_op jit(solution)/shard_map/ppermute | solution.py:279
  180.4 12.8 %collective-permute-start.4 = (f32[2,8,128]{2,1,0:T(8,128)S(1)}, f32[2,8,128]{2,1,0:T(8,128)S(1)}, u32[]{:S(2)}, u32[]{:S(2)}) collective-permute-start(f32[2,8,128]{2,1,0:T(8,128)S(1)} %pad_maximum_fusion), channel_id=1, source_target_pairs={{0,16},{8,24},{16,0},{24,8},{1,17},{9,25},{17,1},{25,9},{2,18},{10... | collective-permute-start | bytes 24584 | tf_op jit(solution)/shard_map/ppermute | solution.py:279
  181.2 12.1 %collective-permute-start.3 = (f32[2,8,128]{2,1,0:T(8,128)S(1)}, f32[2,8,128]{2,1,0:T(8,128)S(1)}, u32[]{:S(2)}, u32[]{:S(2)}) collective-permute-start(f32[2,8,128]{2,1,0:T(8,128)S(1)} %pad_maximum_fusion), channel_id=1, source_target_pairs={{0,8},{8,16},{16,24},{24,0},{1,9},{9,17},{17,25},{25,1},{2,10},{10... | collective-permute-start | bytes 24584 | tf_op jit(solution)/shard_map/ppermute | solution.py:279
  193.2 1.3 collective-permute-start.6
  194.5 4.4 %collective-permute-start.9 = (f32[2,8,128]{2,1,0:T(8,128)S(1)}, f32[2,8,128]{2,1,0:T(8,128)S(1)}, u32[]{:S(2)}, u32[]{:S(2)}) collective-permute-start(f32[2,8,128]{2,1,0:T(8,128)S(1)} %add.45), channel_id=1, source_target_pairs={{0,3},{1,0},{2,1},{3,2},{4,7},{5,4},{6,5},{7,6},{8,11},{9,8},{10,9... | collective-permute-start | bytes 24584 | tf_op jit(solution)/shard_map/ppermute | solution.py:279
  197.2 5.2 %collective-permute-start.8 = (f32[2,8,128]{2,1,0:T(8,128)S(1)}, f32[2,8,128]{2,1,0:T(8,128)S(1)}, u32[]{:S(2)}, u32[]{:S(2)}) collective-permute-start(f32[2,8,128]{2,1,0:T(8,128)S(1)} %add.45), channel_id=1, source_target_pairs={{0,2},{1,3},{2,0},{3,1},{4,6},{5,7},{6,4},{7,5},{8,10},{9,11},{10,... | collective-permute-start | bytes 24584 | tf_op jit(solution)/shard_map/ppermute | solution.py:279
  198.0 4.9 %collective-permute-start.7 = (f32[2,8,128]{2,1,0:T(8,128)S(1)}, f32[2,8,128]{2,1,0:T(8,128)S(1)}, u32[]{:S(2)}, u32[]{:S(2)}) collective-permute-start(f32[2,8,128]{2,1,0:T(8,128)S(1)} %add.45), channel_id=1, source_target_pairs={{0,1},{1,2},{2,3},{3,0},{4,5},{5,6},{6,7},{7,4},{8,9},{9,10},{10,1... | collective-permute-start | bytes 24584 | tf_op jit(solution)/shard_map/ppermute | solution.py:279
  202.9 9.3 %collective-permute-start.16 = (f32[2,8,128]{2,1,0:T(8,128)S(1)}, f32[2,8,128]{2,1,0:T(8,128)S(1)}, u32[]{:S(2)}, u32[]{:S(2)}) collective-permute-start(f32[2,8,128]{2,1,0:T(8,128)S(1)} %add_add_fusion.1), channel_id=1, source_target_pairs={{0,196},{4,0},{64,4},{68,64},{128,68},{132,128},{192,132},{196,192... | collective-permute-start | bytes 24584 | tf_op jit(solution)/shard_map/ppermute | solution.py:279
  203.4 11.0 %collective-permute-start.15 = (f32[2,8,128]{2,1,0:T(8,128)S(1)}, f32[2,8,128]{2,1,0:T(8,128)S(1)}, u32[]{:S(2)}, u32[]{:S(2)}) collective-permute-start(f32[2,8,128]{2,1,0:T(8,128)S(1)} %add_add_fusion.1), channel_id=1, source_target_pairs={{0,192},{4,196},{64,0},{68,4},{128,64},{132,68},{192,128},{196,132... | collective-permute-start | bytes 24584 | tf_op jit(solution)/shard_map/ppermute | solution.py:279
  207.2 9.7 %collective-permute-start.14 = (f32[2,8,128]{2,1,0:T(8,128)S(1)}, f32[2,8,128]{2,1,0:T(8,128)S(1)}, u32[]{:S(2)}, u32[]{:S(2)}) collective-permute-start(f32[2,8,128]{2,1,0:T(8,128)S(1)} %add_add_fusion.1), channel_id=1, source_target_pairs={{0,132},{4,192},{64,196},{68,0},{128,4},{132,64},{192,68},{196,128... | collective-permute-start | bytes 24584 | tf_op jit(solution)/shard_map/ppermute | solution.py:279
  209.4 8.0 %collective-permute-start.13 = (f32[2,8,128]{2,1,0:T(8,128)S(1)}, f32[2,8,128]{2,1,0:T(8,128)S(1)}, u32[]{:S(2)}, u32[]{:S(2)}) collective-permute-start(f32[2,8,128]{2,1,0:T(8,128)S(1)} %add_add_fusion.1), channel_id=1, source_target_pairs={{0,128},{4,132},{64,192},{68,196},{128,0},{132,4},{192,64},{196,68... | collective-permute-start | bytes 24584 | tf_op jit(solution)/shard_map/ppermute | solution.py:279
  212.2 6.7 %collective-permute-start.12 = (f32[2,8,128]{2,1,0:T(8,128)S(1)}, f32[2,8,128]{2,1,0:T(8,128)S(1)}, u32[]{:S(2)}, u32[]{:S(2)}) collective-permute-start(f32[2,8,128]{2,1,0:T(8,128)S(1)} %add_add_fusion.1), channel_id=1, source_target_pairs={{0,68},{4,128},{64,132},{68,192},{128,196},{132,0},{192,4},{196,64... | collective-permute-start | bytes 24584 | tf_op jit(solution)/shard_map/ppermute | solution.py:279
  214.5 5.8 %collective-permute-start.11 = (f32[2,8,128]{2,1,0:T(8,128)S(1)}, f32[2,8,128]{2,1,0:T(8,128)S(1)}, u32[]{:S(2)}, u32[]{:S(2)}) collective-permute-start(f32[2,8,128]{2,1,0:T(8,128)S(1)} %add_add_fusion.1), channel_id=1, source_target_pairs={{0,64},{4,68},{64,128},{68,132},{128,192},{132,196},{192,0},{196,4... | collective-permute-start | bytes 24584 | tf_op jit(solution)/shard_map/ppermute | solution.py:279
  216.9 4.0 %collective-permute-start.10 = (f32[2,8,128]{2,1,0:T(8,128)S(1)}, f32[2,8,128]{2,1,0:T(8,128)S(1)}, u32[]{:S(2)}, u32[]{:S(2)}) collective-permute-start(f32[2,8,128]{2,1,0:T(8,128)S(1)} %add_add_fusion.1), channel_id=1, source_target_pairs={{0,4},{4,64},{64,68},{68,128},{128,132},{132,192},{192,196},{196,0... | collective-permute-start | bytes 24584 | tf_op jit(solution)/shard_map/ppermute | solution.py:279
  217.5 16.5 %collective-permute-start.21 = (f32[128,8,128]{2,1,0:T(8,128)}, f32[128,8,128]{2,1,0:T(8,128)S(1)}, u32[]{:S(2)}, u32[]{:S(2)}) collective-permute-start(f32[128,8,128]{2,1,0:T(8,128)} %get-tuple-element.33), channel_id=1, source_target_pairs={{0,16},{8,24},{16,0},{24,8},{1,17},{9,25},{17,1},{25,9},{2,18},{10... | collective-permute-start | bytes 1572872 | tf_op jit(solution)/shard_map/ppermute | solution.py:279
  218.9 24.2 %collective-permute-start.22 = (f32[128,8,128]{2,1,0:T(8,128)}, f32[128,8,128]{2,1,0:T(8,128)S(1)}, u32[]{:S(2)}, u32[]{:S(2)}) collective-permute-start(f32[128,8,128]{2,1,0:T(8,128)} %get-tuple-element.34), channel_id=1, source_target_pairs={{0,24},{8,0},{16,8},{24,16},{1,25},{9,1},{17,9},{25,17},{2,26},{10... | collective-permute-start | bytes 1572872 | tf_op jit(solution)/shard_map/ppermute | solution.py:279
  220.2 24.9 %collective-permute-start.17 = (f32[128,8,128]{2,1,0:T(8,128)}, f32[128,8,128]{2,1,0:T(8,128)S(1)}, u32[]{:S(2)}, u32[]{:S(2)}) collective-permute-start(f32[128,8,128]{2,1,0:T(8,128)} %get-tuple-element.28), channel_id=1, source_target_pairs={{0,8},{8,16},{16,24},{24,0},{1,9},{9,17},{17,25},{25,1},{2,10},{10... | collective-permute-start | bytes 1572872 | tf_op jit(solution)/shard_map/ppermute | solution.py:279
  220.9 31.1 %collective-permute-start.18 = (f32[128,8,128]{2,1,0:T(8,128)}, f32[128,8,128]{2,1,0:T(8,128)S(1)}, u32[]{:S(2)}, u32[]{:S(2)}) collective-permute-start(f32[128,8,128]{2,1,0:T(8,128)} %get-tuple-element.29), channel_id=1, source_target_pairs={{0,16},{8,24},{16,0},{24,8},{1,17},{9,25},{17,1},{25,9},{2,18},{10... | collective-permute-start | bytes 1572872 | tf_op jit(solution)/shard_map/ppermute | solution.py:279
  223.0 38.1 %collective-permute-start.19 = (f32[128,8,128]{2,1,0:T(8,128)}, f32[128,8,128]{2,1,0:T(8,128)S(1)}, u32[]{:S(2)}, u32[]{:S(2)}) collective-permute-start(f32[128,8,128]{2,1,0:T(8,128)} %get-tuple-element.30), channel_id=1, source_target_pairs={{0,24},{8,0},{16,8},{24,16},{1,25},{9,1},{17,9},{25,17},{2,26},{10... | collective-permute-start | bytes 1572872 | tf_op jit(solution)/shard_map/ppermute | solution.py:279

commit v2 on v1

--- a/solution.py
+++ b/solution.py
@@ -210,36 +210,71 @@
         o[...] = (mm(bh, hi) + (mm(bh, lo) + mm(bl, hi))).reshape(o.shape)
 
 
-def last_kernel(me_ref, sum_ref, v_ref, h_ref, *refs):
-    n_y = (len(refs) - 7) // 2
-    pieces, o_ref = refs[: 2 * n_y], refs[2 * n_y]
-    v_buf, h_buf, p_buf, o_buf, in_sem, out_sem = refs[2 * n_y + 1 :]
+def step_length(sum_ref):
+    size_field, size_first = jnp.sum(sum_ref[0]), jnp.sum(sum_ref[1])
+    ratio = size_field / (jnp.full((1, 128), size_first, f32) + epsilon)
+    return (target_ratio * jnp.sqrt(ratio)).reshape(1, 1, 128)
+
+
+def home_rows(me_ref, d, n_y, sub):
+    return pl.ds(pl.multiple_of(lax.rem(me_ref[0] + n_y - d, n_y) * sub, sub), sub)
+
+
+def most_kernel(me_ref, sum_ref, v_ref, h_ref, cross_ref, *refs):
+    *pieces, o_ref, most_ref, v_buf, h_buf, p_buf, c_buf, o_buf, in_sem, out_sem = refs
+    n_y = len(pieces)
     sub = v_buf.shape[1]
-    loads, stores = [], []
+    loads = []
     for d in range(n_y):
-        k = pl.ds(pl.multiple_of(lax.rem(me_ref[0] + n_y - d, n_y) * sub, sub), sub)
-        parts = (
-            (pieces[d], p_buf.at[d, 0]),
-            (pieces[n_y + d], p_buf.at[d, 1]),
+        k = home_rows(me_ref, d, n_y, sub)
+        parts = [
+            (pieces[d], p_buf.at[d]),
             (v_ref.at[k], v_buf.at[d]),
             (h_ref.at[:, k], h_buf.at[d]),
-        )
+        ]
+        if d == 0:
+            parts.append((cross_ref, c_buf))
         loads.append(
             [pltpu.make_async_copy(a, b, in_sem.at[d, i]) for i, (a, b) in enumerate(parts)]
         )
-        stores.append(pltpu.make_async_copy(o_buf.at[d], o_ref.at[k], out_sem.at[d]))
         for load in loads[-1]:
             load.start()
-    size_field, size_first = jnp.sum(sum_ref[0]), jnp.sum(sum_ref[1])
-    ratio = size_field / (jnp.full((1, 128), size_first, f32) + epsilon)
-    step = (target_ratio * jnp.sqrt(ratio)).reshape(1, 1, 128)
+    step = step_length(sum_ref)
+    store = pltpu.make_async_copy(o_buf, o_ref.at[home_rows(me_ref, 0, n_y, sub)], out_sem.at[0])
     for d in range(n_y):
         for load in loads[d]:
             load.wait()
-        value = (step * step / 2.0) * (p_buf[d, 1] + h_buf[d]) - step * p_buf[d, 0]
+        second = h_buf[d] + c_buf[...] if d == 0 else h_buf[d]
+        value = (step * step / 2.0) * second - step * p_buf[d]
         for k in range(sub):
-            o_buf[d, k] = v_buf[d, k] + value[:, k].T
-        stores[d].start()
+            row = v_buf[d, k] + value[:, k].T
+            if d == 0:
+                o_buf[k] = row
+            else:
+                most_ref[d - 1, k] = row
+        if d == 0:
+            store.start()
+    store.wait()
+
+
+def last_kernel(me_ref, sum_ref, most_ref, part_ref, *refs):
+    n_y, sub = most_ref.shape[0] + 1, most_ref.shape[1]
+    pieces, (o_ref, p_buf, o_buf, in_sem, out_sem) = refs[: n_y - 1], refs[n_y - 1 :]
+    loads = [
+        pltpu.make_async_copy(p, p_buf.at[d], in_sem.at[d]) for d, p in enumerate(pieces)
+    ]
+    for load in loads:
+        load.start()
+    step = step_length(sum_ref)
+    stores = []
+    for d in range(n_y - 1):
+        loads[d].wait()
+        value = (step * step / 2.0) * p_buf[d]
+        for k in range(sub):
+            o_buf[d, k] = most_ref[d, k] + value[:, k].T
+        k = home_rows(me_ref, d + 1, n_y, sub)
+        stores.append(pltpu.make_async_copy(o_buf.at[d], o_ref.at[k], out_sem.at[d]))
+        stores[-1].start()
     for store in stores:
         store.wait()
 
@@ -248,22 +283,40 @@
     n_y = len(crosses)
     depth, rows, cols = field.shape
     sub = depth // n_y
-    block, turned = (n_y, sub, rows, cols), (n_y, cols, sub, rows)
+    block, turned = (sub, rows, cols), (cols, sub, rows)
+    part, most = pl.pallas_call(
+        most_kernel,
+        compiler_params=LIMIT,
+        in_specs=[SMEM, VMEM, IN_HBM, ANY, IN_HBM, IN_HBM] + [ANY] * (n_y - 1),
+        out_specs=[IN_HBM, VMEM],
+        out_shape=[
+            HBM(field.shape, f32),
+            jax.ShapeDtypeStruct((n_y - 1,) + block, f32),
+        ],
+        scratch_shapes=[
+            pltpu.VMEM((n_y,) + block, f32),
+            pltpu.VMEM((n_y,) + turned, f32),
+            pltpu.VMEM((n_y,) + turned, f32),
+            pltpu.VMEM(turned, f32),
+            pltpu.VMEM(block, f32),
+            pltpu.SemaphoreType.DMA((n_y, 4)),
+            pltpu.SemaphoreType.DMA((1,)),
+        ],
+    )(me, sums, far(field), far(h), far(crosses[0]), far(firsts[0]), *firsts[1:])
     return pl.pallas_call(
         last_kernel,
         compiler_params=LIMIT,
-        in_specs=[SMEM, VMEM, IN_HBM, ANY] + ([IN_HBM] + [ANY] * (n_y - 1)) * 2,
-        out_specs=ANY,
-        out_shape=jax.ShapeDtypeStruct(field.shape, f32),
+        in_specs=[SMEM, VMEM, VMEM, IN_HBM] + [ANY] * (n_y - 1),
+        out_specs=IN_HBM,
+        out_shape=HBM(field.shape, f32),
+        input_output_aliases={3: 0},
         scratch_shapes=[
-            pltpu.VMEM(block, f32),
-            pltpu.VMEM(turned, f32),
-            pltpu.VMEM((n_y, 2) + turned[1:], f32),
-            pltpu.VMEM(block, f32),
-            pltpu.SemaphoreType.DMA((n_y, 4)),
-            pltpu.SemaphoreType.DMA((n_y,)),
+            pltpu.VMEM((n_y - 1,) + turned, f32),
+            pltpu.VMEM((n_y - 1,) + block, f32),
+            pltpu.SemaphoreType.DMA((n_y - 1,)),
+            pltpu.SemaphoreType.DMA((n_y - 1,)),
         ],
-    )(me, sums, far(field), far(h), far(firsts[0]), *firsts[1:], far(crosses[0]), *crosses[1:])
+    )(me, sums, most, part, *crosses[1:])
 
 
 def on_device(field, factor_a, factor_b, factor_c):
@@ -279,7 +332,10 @@
         return lax.ppermute(value, axis, [(i, (i + d) % n) for i in range(n)])
 
     def exchanged(pieces, axis):
-        return [shifted(p, axis, d) if d else p for d, p in enumerate(pieces)]
+        out = list(pieces)
+        for d in sorted(range(1, len(pieces)), key=lambda d: min(d, len(pieces) - d)):
+            out[d] = shifted(pieces[d], axis, d)
+        return out
 
     def all_to_all(value, axes):
         value = value.reshape((-1,) + value.shape[-2:])

time: 268 us -> 268 us (level)
  waiting for transfers between devices: 166 us -> 157 us
  local copies, waits for them, and re-layouts: 6.84 us -> 12.4 us
  starting transfers between devices: 60.6 us -> 63.5 us
    ppermute x23, waiting for transfers between devices: 78.7 us -> 69.5 us  [shifted(): return lax.ppermute(value, axis, [(i, (i + d) % n) for i in range(n)])]
    unnamed x9 -> x21, local copies, waits for them, and re-layouts: 6.84 us -> 12.4 us
    pallas_call x0 -> x1, Pallas kernels: none -> 3.37 us  [last_step(): pl.pallas_call(most_kernel, compiler_params=LIMIT, in_specs=[SMEM, VMEM,...]
    ppermute x23, starting transfers between devices: 32.3 us -> 35 us  [shifted(): return lax.ppermute(value, axis, [(i, (i + d) % n) for i in range(n)])]
  transfers between devices with their start and end apart: 26 -> 26, of which waited for: 15 -> 11; matrix products, arithmetic and copies ran while one was open for 0% -> 0% of each run, Pallas kernels for 7% -> 9%
where the time goes in v2:
time: 268 us; the launch traced here: 267 us
  waiting for transfers between devices  157 us (59%)
  starting transfers between devices  63.5 us (24%)
  Pallas kernels  33.6 us (13%)
  local copies, waits for them, and re-layouts  12.4 us (5%)
    all_to_all x3, waiting for transfers between devices, all_to_all(): return lax.all_to_all(value, axes, 0, 0, tiled=True)  87.3 us
    ppermute x23, waiting for transfers between devices, shifted(): return lax.ppermute(value, axis, [(i, (i + d) % n) for i in range(n)])  69.5 us
    ppermute x23, starting transfers between devices, shifted(): return lax.ppermute(value, axis, [(i, (i + d) % n) for i in range(n)])  35 us
    all_to_all x3, starting transfers between devices, all_to_all(): return lax.all_to_all(value, axes, 0, 0, tiled=True)  28.5 us
    pallas_call x2, Pallas kernels, planes_call(): pl.pallas_call(kernel, compiler_params=LIMIT, grid=(n_zh,), in_specs=[who...  16 us
    unnamed x21, local copies, waits for them, and re-layouts  12.4 us
    pallas_call x4, Pallas kernels, call(): pl.pallas_call(kernel, compiler_params=LIMIT, out_shape=[HBM(s, f32) if o...  8.73 us
  transfers between devices with their start and end apart: 26, of which 11 were waited for; matrix products, arithmetic and copies ran while one was open for 0% of the time, Pallas kernels for 9%

profile of v2, /device:TPU:32, one launch (start us, length us, event | category | flops | bytes accessed | tf_op | source)
XLA Modules:
  0.0 266.7 jit_solution(3285034207588923282)
XLA Ops:
  0.0 3.0 %copy.6 = f32[32,128,128]{1,0,2:T(8,128)} copy(f32[32,128,128]{2,1,0:T(8,128)} %v_ref.1) | data formatting | bytes 4194304 | tf_op args[0]
  3.0 11.9 %all-to-all-start = ((f32[128,32,128]{2,1,0:T(8,128)}), f32[128,32,128]{2,1,0:T(8,128)}, u32[]{:S(2)}, u32[]{:S(2)}) async-start(f32[128,32,128]{2,1,0:T(8,128)} %bitcast.1.v_ref), calls=%async_computation | async-start | bytes 4194304 | tf_op jit(solution)/shard_map/all_to_all | solution.py:342
  15.0 2.2 copy-done.1
  17.2 3.0 %shard_map.49.at_ref = bf16[4,2,1024,256]{3,2,1,0:T(8,128)(2,1)} custom-call(f32[1024,1024]{1,0:T(8,128)S(1)} %copy-done.1), custom_call_target="tpu_custom_call" | custom-call | tf_op jit(solution)/shard_map/pallas_call | solution.py:54
  20.2 44.3 %all-to-all-done = f32[128,32,128]{2,1,0:T(8,128)} async-done(((f32[128,32,128]{2,1,0:T(8,128)}), f32[128,32,128]{2,1,0:T(8,128)}, u32[]{:S(2)}, u32[]{:S(2)}) %all-to-all-start) | async-done | bytes 2097184 | tf_op jit(solution)/shard_map/all_to_all | solution.py:342
  64.5 8.3 %shard_map.51.g_ref = f32[4,2,4,2,4,2,8,128]{7,6,5,4,3,2,1,0:T(8,128)} custom-call(f32[2,4,2,4,2,32,128]{6,5,4,3,2,1,0:T(8,128)} %bitcast.3.v_ref, bf16[4,2,1024,256]{3,2,1,0:T(8,128)(2,1)} %shard_map.49.at_ref, bf16[2,256,256]{2,1,0:T(8,128)(2,1)S(1)} %shard_map.50.c_ref), custom_call_target="tpu_custom_call" | custom-call | tf_op jit(solution)/shard_map/pallas_call | solution.py:159
  72.9 9.9 %all-to-all-start.1 = ((f32[512,8,128]{2,1,0:T(8,128)}), f32[512,8,128]{2,1,0:T(8,128)S(1)}, u32[]{:S(2)}, u32[]{:S(2)}) async-start(f32[512,8,128]{2,1,0:T(8,128)} %bitcast.10), calls=%async_computation.1 | async-start | bytes 4194304 | tf_op jit(solution)/shard_map/all_to_all | solution.py:342
  82.8 1.6 copy-done
  84.4 7.6 %shard_map.53 = f32[2,4,2,4,2,32,128]{6,5,4,3,2,1,0:T(8,128)} custom-call(f32[4,2,4,2,4,2,8,128]{7,6,5,4,3,2,1,0:T(8,128)S(1)} %copy-done, bf16[4,2,1024,256]{3,2,1,0:T(8,128)(2,1)} %shard_map.49.at_ref, bf16[2,256,256]{2,1,0:T(8,128)(2,1)S(1)} %shard_map.50.c_ref), custom_call_target="tpu_custom_call" | custom-call | tf_op jit(solution)/shard_map/pallas_call | solution.py:159
  92.0 43.0 %all-to-all-done.1 = f32[512,8,128]{2,1,0:T(8,128)S(1)} async-done(((f32[512,8,128]{2,1,0:T(8,128)}), f32[512,8,128]{2,1,0:T(8,128)S(1)}, u32[]{:S(2)}, u32[]{:S(2)}) %all-to-all-start.1) | async-done | bytes 2097184 | tf_op jit(solution)/shard_map/all_to_all | solution.py:342
  135.0 6.7 %all-to-all-start.2 = ((f32[128,32,128]{2,1,0:T(8,128)}), f32[128,32,128]{2,1,0:T(8,128)}, u32[]{:S(2)}, u32[]{:S(2)}) async-start(f32[128,32,128]{2,1,0:T(8,128)} %bitcast.15), calls=%async_computation.2 | async-start | bytes 4194304 | tf_op jit(solution)/shard_map/all_to_all | solution.py:342
  141.8 2.0 shard_map.46
  144.4 1.9 collective-permute-start.1
  147.6 22.7 %collective-permute-done.refs_1_ = f32[128,8,128]{2,1,0:T(8,128)S(1)} collective-permute-done((f32[128,8,128]{2,1,0:T(8,128)S(1)}, f32[128,8,128]{2,1,0:T(8,128)S(1)}, u32[]{:S(2)}, u32[]{:S(2)}) %collective-permute-start) | collective-permute-done | bytes 524320 | tf_op jit(solution)/shard_map/ppermute | solution.py:332
  170.9 2.2 shard_map.48
  174.9 2.8 %collective-permute-start.5 = (f32[2,8,128]{2,1,0:T(8,128)S(1)}, f32[2,8,128]{2,1,0:T(8,128)S(1)}, u32[]{:S(2)}, u32[]{:S(2)}) collective-permute-start(f32[2,8,128]{2,1,0:T(8,128)S(1)} %pad_maximum_fusion), channel_id=1, source_target_pairs={{0,24},{8,0},{16,8},{24,16},{1,25},{9,1},{17,9},{25,17},{2,26},{10... | collective-permute-start | bytes 24584 | tf_op jit(solution)/shard_map/ppermute | solution.py:332
  178.4 1.4 collective-permute-start.3
  179.9 10.6 %collective-permute-done.4 = f32[2,8,128]{2,1,0:T(8,128)S(1)} collective-permute-done((f32[2,8,128]{2,1,0:T(8,128)S(1)}, f32[2,8,128]{2,1,0:T(8,128)S(1)}, u32[]{:S(2)}, u32[]{:S(2)}) %collective-permute-start.4) | collective-permute-done | bytes 8224 | tf_op jit(solution)/shard_map/ppermute | solution.py:332
  191.8 2.7 %collective-permute-start.9 = (f32[2,8,128]{2,1,0:T(8,128)S(1)}, f32[2,8,128]{2,1,0:T(8,128)S(1)}, u32[]{:S(2)}, u32[]{:S(2)}) collective-permute-start(f32[2,8,128]{2,1,0:T(8,128)S(1)} %add.45), channel_id=1, source_target_pairs={{0,3},{1,0},{2,1},{3,2},{4,7},{5,4},{6,5},{7,6},{8,11},{9,8},{10,9... | collective-permute-start | bytes 24584 | tf_op jit(solution)/shard_map/ppermute | solution.py:332
  196.2 3.5 %collective-permute-done.8 = f32[2,8,128]{2,1,0:T(8,128)S(1)} collective-permute-done((f32[2,8,128]{2,1,0:T(8,128)S(1)}, f32[2,8,128]{2,1,0:T(8,128)S(1)}, u32[]{:S(2)}, u32[]{:S(2)}) %collective-permute-start.8) | collective-permute-done | bytes 8224 | tf_op jit(solution)/shard_map/ppermute | solution.py:332
  200.7 3.7 %collective-permute-start.15 = (f32[2,8,128]{2,1,0:T(8,128)S(1)}, f32[2,8,128]{2,1,0:T(8,128)S(1)}, u32[]{:S(2)}, u32[]{:S(2)}) collective-permute-start(f32[2,8,128]{2,1,0:T(8,128)S(1)} %add_add_fusion.1), channel_id=1, source_target_pairs={{0,192},{4,196},{64,0},{68,4},{128,64},{132,68},{192,128},{196,132... | collective-permute-start | bytes 24584 | tf_op jit(solution)/shard_map/ppermute | solution.py:332
  204.5 2.3 collective-permute-start.14
  206.7 2.8 %collective-permute-start.13 = (f32[2,8,128]{2,1,0:T(8,128)S(1)}, f32[2,8,128]{2,1,0:T(8,128)S(1)}, u32[]{:S(2)}, u32[]{:S(2)}) collective-permute-start(f32[2,8,128]{2,1,0:T(8,128)S(1)} %add_add_fusion.1), channel_id=1, source_target_pairs={{0,128},{4,132},{64,192},{68,196},{128,0},{132,4},{192,64},{196,68... | collective-permute-start | bytes 24584 | tf_op jit(solution)/shard_map/ppermute | solution.py:332
  209.5 2.2 collective-permute-start.12
  211.7 2.4 collective-permute-start.11
  214.8 3.3 %shard_map.54 = (f32[128,8,128]{2,1,0:T(8,128)}, f32[128,8,128]{2,1,0:T(8,128)}, f32[128,8,128]{2,1,0:T(8,128)}, f32[128,8,128]{2,1,0:T(8,128)}) custom-call(s32[1]{0:T(128)} %bitcast.me_ref, f32[4,128,8,128]{3,2,1,0:T(8,128)S(1)} %get-tuple-element.27.bv_ref, f32[4,128,8,128]{3,2,1,0:T(8,128)S(1)} %bitcast.9, bf16[2,512,512]{2,1,0:T(8,128)(2,1)S(1)} %shard_map.47.refs_4_.b_ref), custom_call_target="tpu_custom_call" | custom-call | tf_op jit(solution)/shard_map/pallas_call | solution.py:67
  218.0 2.0 collective-permute-start.18
  221.3 2.8 %collective-permute-start.21 = (f32[128,8,128]{2,1,0:T(8,128)}, f32[128,8,128]{2,1,0:T(8,128)S(1)}, u32[]{:S(2)}, u32[]{:S(2)}) collective-permute-start(f32[128,8,128]{2,1,0:T(8,128)} %get-tuple-element.37), channel_id=1, source_target_pairs={{0,16},{8,24},{16,0},{24,8},{1,17},{9,25},{17,1},{25,9},{2,18},{10... | collective-permute-start | bytes 1572872 | tf_op jit(solution)/shard_map/ppermute | solution.py:332
  225.7 18.6 %collective-permute-done.18.refs_2_ = f32[128,8,128]{2,1,0:T(8,128)S(1)} collective-permute-done((f32[128,8,128]{2,1,0:T(8,128)}, f32[128,8,128]{2,1,0:T(8,128)S(1)}, u32[]{:S(2)}, u32[]{:S(2)}) %collective-permute-start.18) | collective-permute-done | bytes 524320 | tf_op jit(solution)/shard_map/ppermute | solution.py:332
  250.3 3.4 %shard_map.55 = (f32[32,128,128]{2,1,0:T(8,128)}, f32[3,8,128,128]{3,2,1,0:T(8,128)S(1)}) custom-call(s32[1]{0:T(128)} %bitcast.me_ref, f32[2,8,128]{2,1,0:T(8,128)S(1)} %add_add_fusion.sum_ref, f32[32,128,128]{2,1,0:T(8,128)} %v_ref.1, f32[128,32,128]{2,1,0:T(8,128)} %all-to-all-done.2.h_ref, f32[128,8,128]{2,1,0:T(8,128)} %get-tuple-element.29.cross_ref, ...), custom_call_target="tpu_custom_call" | custom-call | tf_op jit(solution)/shard_map/pallas_call | solution.py:287
  253.7 10.5 %collective-permute-done.22.refs_2_ = f32[128,8,128]{2,1,0:T(8,128)} collective-permute-done((f32[128,8,128]{2,1,0:T(8,128)}, f32[128,8,128]{2,1,0:T(8,128)}, u32[]{:S(2)}, u32[]{:S(2)}) %collective-permute-start.22) | collective-permute-done | bytes 524320 | tf_op jit(solution)/shard_map/ppermute | solution.py:332
  264.2 2.3 shard_map.56
  (57 shorter events, 18.5 us)
Async XLA Ops:
  3.0 11.9 %copy-start.9 = (f32[256,256]{1,0:T(8,128)S(1)}, f32[256,256]{1,0:T(8,128)}, u32[]{:S(2)}) copy-start(f32[256,256]{1,0:T(8,128)} %x_ref.5) | copy-start | bytes 786436
  3.0 61.5 %all-to-all-start = ((f32[128,32,128]{2,1,0:T(8,128)}), f32[128,32,128]{2,1,0:T(8,128)}, u32[]{:S(2)}, u32[]{:S(2)}) async-start(f32[128,32,128]{2,1,0:T(8,128)} %bitcast.1.v_ref), calls=%async_computation | async-start | bytes 4194304 | tf_op jit(solution)/shard_map/all_to_all | solution.py:342
  15.0 2.2 copy-start.1
  72.9 62.1 %all-to-all-start.1 = ((f32[512,8,128]{2,1,0:T(8,128)}), f32[512,8,128]{2,1,0:T(8,128)S(1)}, u32[]{:S(2)}, u32[]{:S(2)}) async-start(f32[512,8,128]{2,1,0:T(8,128)} %bitcast.10), calls=%async_computation.1 | async-start | bytes 4194304 | tf_op jit(solution)/shard_map/all_to_all | solution.py:342
  82.7 1.6 copy-start
  135.0 90.7 %all-to-all-start.2 = ((f32[128,32,128]{2,1,0:T(8,128)}), f32[128,32,128]{2,1,0:T(8,128)}, u32[]{:S(2)}, u32[]{:S(2)}) async-start(f32[128,32,128]{2,1,0:T(8,128)} %bitcast.15), calls=%async_computation.2 | async-start | bytes 4194304 | tf_op jit(solution)/shard_map/all_to_all | solution.py:342
  141.8 5.7 %copy-start.2 = (f32[512,512]{1,0:T(8,128)S(1)}, f32[512,512]{1,0:T(8,128)}, u32[]{:S(2)}) copy-start(f32[512,512]{1,0:T(8,128)} %x_ref.3) | copy-start | bytes 3145732
  143.7 26.6 %collective-permute-start = (f32[128,8,128]{2,1,0:T(8,128)S(1)}, f32[128,8,128]{2,1,0:T(8,128)S(1)}, u32[]{:S(2)}, u32[]{:S(2)}) collective-permute-start(f32[128,8,128]{2,1,0:T(8,128)S(1)} %get-tuple-element.23), channel_id=1, source_target_pairs={{0,8},{8,16},{16,24},{24,0},{1,9},{9,17},{17,25},{25,1},{2,10},{10... | collective-permute-start | bytes 1572872 | tf_op jit(solution)/shard_map/ppermute | solution.py:332
  144.4 25.9 %collective-permute-start.1 = (f32[128,8,128]{2,1,0:T(8,128)S(1)}, f32[128,8,128]{2,1,0:T(8,128)S(1)}, u32[]{:S(2)}, u32[]{:S(2)}) collective-permute-start(f32[128,8,128]{2,1,0:T(8,128)S(1)} %get-tuple-element.24), channel_id=1, source_target_pairs={{0,16},{8,24},{16,0},{24,8},{1,17},{9,25},{17,1},{25,9},{2,18},{10... | collective-permute-start | bytes 1572872 | tf_op jit(solution)/shard_map/ppermute | solution.py:332
  146.4 24.6 %collective-permute-start.2 = (f32[128,8,128]{2,1,0:T(8,128)S(1)}, f32[128,8,128]{2,1,0:T(8,128)S(1)}, u32[]{:S(2)}, u32[]{:S(2)}) collective-permute-start(f32[128,8,128]{2,1,0:T(8,128)S(1)} %get-tuple-element.25), channel_id=1, source_target_pairs={{0,24},{8,0},{16,8},{24,16},{1,25},{9,1},{17,9},{25,17},{2,26},{10... | collective-permute-start | bytes 1572872 | tf_op jit(solution)/shard_map/ppermute | solution.py:332
  174.5 49.7 %collective-permute-start.17 = (f32[128,8,128]{2,1,0:T(8,128)S(1)}, f32[128,8,128]{2,1,0:T(8,128)S(1)}, u32[]{:S(2)}, u32[]{:S(2)}) collective-permute-start(f32[128,8,128]{2,1,0:T(8,128)S(1)} %get-tuple-element.31), channel_id=1, source_target_pairs={{0,8},{8,16},{16,24},{24,0},{1,9},{9,17},{17,25},{25,1},{2,10},{10... | collective-permute-start | bytes 1572872 | tf_op jit(solution)/shard_map/ppermute | solution.py:332
  174.9 5.0 %collective-permute-start.5 = (f32[2,8,128]{2,1,0:T(8,128)S(1)}, f32[2,8,128]{2,1,0:T(8,128)S(1)}, u32[]{:S(2)}, u32[]{:S(2)}) collective-permute-start(f32[2,8,128]{2,1,0:T(8,128)S(1)} %pad_maximum_fusion), channel_id=1, source_target_pairs={{0,24},{8,0},{16,8},{24,16},{1,25},{9,1},{17,9},{25,17},{2,26},{10... | collective-permute-start | bytes 24584 | tf_op jit(solution)/shard_map/ppermute | solution.py:332
  177.7 12.8 %collective-permute-start.4 = (f32[2,8,128]{2,1,0:T(8,128)S(1)}, f32[2,8,128]{2,1,0:T(8,128)S(1)}, u32[]{:S(2)}, u32[]{:S(2)}) collective-permute-start(f32[2,8,128]{2,1,0:T(8,128)S(1)} %pad_maximum_fusion), channel_id=1, source_target_pairs={{0,16},{8,24},{16,0},{24,8},{1,17},{9,25},{17,1},{25,9},{2,18},{10... | collective-permute-start | bytes 24584 | tf_op jit(solution)/shard_map/ppermute | solution.py:332
  178.4 12.1 %collective-permute-start.3 = (f32[2,8,128]{2,1,0:T(8,128)S(1)}, f32[2,8,128]{2,1,0:T(8,128)S(1)}, u32[]{:S(2)}, u32[]{:S(2)}) collective-permute-start(f32[2,8,128]{2,1,0:T(8,128)S(1)} %pad_maximum_fusion), channel_id=1, source_target_pairs={{0,8},{8,16},{16,24},{24,0},{1,9},{9,17},{17,25},{25,1},{2,10},{10... | collective-permute-start | bytes 24584 | tf_op jit(solution)/shard_map/ppermute | solution.py:332
  190.5 1.3 collective-permute-start.6
  191.8 4.4 %collective-permute-start.9 = (f32[2,8,128]{2,1,0:T(8,128)S(1)}, f32[2,8,128]{2,1,0:T(8,128)S(1)}, u32[]{:S(2)}, u32[]{:S(2)}) collective-permute-start(f32[2,8,128]{2,1,0:T(8,128)S(1)} %add.45), channel_id=1, source_target_pairs={{0,3},{1,0},{2,1},{3,2},{4,7},{5,4},{6,5},{7,6},{8,11},{9,8},{10,9... | collective-permute-start | bytes 24584 | tf_op jit(solution)/shard_map/ppermute | solution.py:332
  194.5 5.2 %collective-permute-start.8 = (f32[2,8,128]{2,1,0:T(8,128)S(1)}, f32[2,8,128]{2,1,0:T(8,128)S(1)}, u32[]{:S(2)}, u32[]{:S(2)}) collective-permute-start(f32[2,8,128]{2,1,0:T(8,128)S(1)} %add.45), channel_id=1, source_target_pairs={{0,2},{1,3},{2,0},{3,1},{4,6},{5,7},{6,4},{7,5},{8,10},{9,11},{10,... | collective-permute-start | bytes 24584 | tf_op jit(solution)/shard_map/ppermute | solution.py:332
  195.3 4.9 %collective-permute-start.7 = (f32[2,8,128]{2,1,0:T(8,128)S(1)}, f32[2,8,128]{2,1,0:T(8,128)S(1)}, u32[]{:S(2)}, u32[]{:S(2)}) collective-permute-start(f32[2,8,128]{2,1,0:T(8,128)S(1)} %add.45), channel_id=1, source_target_pairs={{0,1},{1,2},{2,3},{3,0},{4,5},{5,6},{6,7},{7,4},{8,9},{9,10},{10,1... | collective-permute-start | bytes 24584 | tf_op jit(solution)/shard_map/ppermute | solution.py:332
  200.2 9.3 %collective-permute-start.16 = (f32[2,8,128]{2,1,0:T(8,128)S(1)}, f32[2,8,128]{2,1,0:T(8,128)S(1)}, u32[]{:S(2)}, u32[]{:S(2)}) collective-permute-start(f32[2,8,128]{2,1,0:T(8,128)S(1)} %add_add_fusion.1), channel_id=1, source_target_pairs={{0,196},{4,0},{64,4},{68,64},{128,68},{132,128},{192,132},{196,192... | collective-permute-start | bytes 24584 | tf_op jit(solution)/shard_map/ppermute | solution.py:332
  200.7 11.0 %collective-permute-start.15 = (f32[2,8,128]{2,1,0:T(8,128)S(1)}, f32[2,8,128]{2,1,0:T(8,128)S(1)}, u32[]{:S(2)}, u32[]{:S(2)}) collective-permute-start(f32[2,8,128]{2,1,0:T(8,128)S(1)} %add_add_fusion.1), channel_id=1, source_target_pairs={{0,192},{4,196},{64,0},{68,4},{128,64},{132,68},{192,128},{196,132... | collective-permute-start | bytes 24584 | tf_op jit(solution)/shard_map/ppermute | solution.py:332
  204.5 9.7 %collective-permute-start.14 = (f32[2,8,128]{2,1,0:T(8,128)S(1)}, f32[2,8,128]{2,1,0:T(8,128)S(1)}, u32[]{:S(2)}, u32[]{:S(2)}) collective-permute-start(f32[2,8,128]{2,1,0:T(8,128)S(1)} %add_add_fusion.1), channel_id=1, source_target_pairs={{0,132},{4,192},{64,196},{68,0},{128,4},{132,64},{192,68},{196,128... | collective-permute-start | bytes 24584 | tf_op jit(solution)/shard_map/ppermute | solution.py:332
  206.7 11.3 %collective-permute-start.13 = (f32[2,8,128]{2,1,0:T(8,128)S(1)}, f32[2,8,128]{2,1,0:T(8,128)S(1)}, u32[]{:S(2)}, u32[]{:S(2)}) collective-permute-start(f32[2,8,128]{2,1,0:T(8,128)S(1)} %add_add_fusion.1), channel_id=1, source_target_pairs={{0,128},{4,132},{64,192},{68,196},{128,0},{132,4},{192,64},{196,68... | collective-permute-start | bytes 24584 | tf_op jit(solution)/shard_map/ppermute | solution.py:332
  209.5 8.5 %collective-permute-start.12 = (f32[2,8,128]{2,1,0:T(8,128)S(1)}, f32[2,8,128]{2,1,0:T(8,128)S(1)}, u32[]{:S(2)}, u32[]{:S(2)}) collective-permute-start(f32[2,8,128]{2,1,0:T(8,128)S(1)} %add_add_fusion.1), channel_id=1, source_target_pairs={{0,68},{4,128},{64,132},{68,192},{128,196},{132,0},{192,4},{196,64... | collective-permute-start | bytes 24584 | tf_op jit(solution)/shard_map/ppermute | solution.py:332
  211.7 8.3 %collective-permute-start.11 = (f32[2,8,128]{2,1,0:T(8,128)S(1)}, f32[2,8,128]{2,1,0:T(8,128)S(1)}, u32[]{:S(2)}, u32[]{:S(2)}) collective-permute-start(f32[2,8,128]{2,1,0:T(8,128)S(1)} %add_add_fusion.1), channel_id=1, source_target_pairs={{0,64},{4,68},{64,128},{68,132},{128,192},{132,196},{192,0},{196,4... | collective-permute-start | bytes 24584 | tf_op jit(solution)/shard_map/ppermute | solution.py:332
  214.2 7.2 %collective-permute-start.10 = (f32[2,8,128]{2,1,0:T(8,128)S(1)}, f32[2,8,128]{2,1,0:T(8,128)S(1)}, u32[]{:S(2)}, u32[]{:S(2)}) collective-permute-start(f32[2,8,128]{2,1,0:T(8,128)S(1)} %add_add_fusion.1), channel_id=1, source_target_pairs={{0,4},{4,64},{64,68},{68,128},{128,132},{132,192},{192,196},{196,0... | collective-permute-start | bytes 24584 | tf_op jit(solution)/shard_map/ppermute | solution.py:332
  218.0 35.7 %collective-permute-start.20 = (f32[128,8,128]{2,1,0:T(8,128)}, f32[128,8,128]{2,1,0:T(8,128)S(1)}, u32[]{:S(2)}, u32[]{:S(2)}) collective-permute-start(f32[128,8,128]{2,1,0:T(8,128)} %get-tuple-element.36), channel_id=1, source_target_pairs={{0,8},{8,16},{16,24},{24,0},{1,9},{9,17},{17,25},{25,1},{2,10},{10... | collective-permute-start | bytes 1572872 | tf_op jit(solution)/shard_map/ppermute | solution.py:332
  218.0 26.3 %collective-permute-start.18 = (f32[128,8,128]{2,1,0:T(8,128)}, f32[128,8,128]{2,1,0:T(8,128)S(1)}, u32[]{:S(2)}, u32[]{:S(2)}) collective-permute-start(f32[128,8,128]{2,1,0:T(8,128)} %get-tuple-element.32), channel_id=1, source_target_pairs={{0,16},{8,24},{16,0},{24,8},{1,17},{9,25},{17,1},{25,9},{2,18},{10... | collective-permute-start | bytes 1572872 | tf_op jit(solution)/shard_map/ppermute | solution.py:332
  220.0 26.3 %collective-permute-start.19 = (f32[128,8,128]{2,1,0:T(8,128)}, f32[128,8,128]{2,1,0:T(8,128)S(1)}, u32[]{:S(2)}, u32[]{:S(2)}) collective-permute-start(f32[128,8,128]{2,1,0:T(8,128)} %get-tuple-element.33), channel_id=1, source_target_pairs={{0,24},{8,0},{16,8},{24,16},{1,25},{9,1},{17,9},{25,17},{2,26},{10... | collective-permute-start | bytes 1572872 | tf_op jit(solution)/shard_map/ppermute | solution.py:332
  221.3 32.3 %collective-permute-start.21 = (f32[128,8,128]{2,1,0:T(8,128)}, f32[128,8,128]{2,1,0:T(8,128)S(1)}, u32[]{:S(2)}, u32[]{:S(2)}) collective-permute-start(f32[128,8,128]{2,1,0:T(8,128)} %get-tuple-element.37), channel_id=1, source_target_pairs={{0,16},{8,24},{16,0},{24,8},{1,17},{9,25},{17,1},{25,9},{2,18},{10... | collective-permute-start | bytes 1572872 | tf_op jit(solution)/shard_map/ppermute | solution.py:332
  225.0 39.2 %collective-permute-start.22 = (f32[128,8,128]{2,1,0:T(8,128)}, f32[128,8,128]{2,1,0:T(8,128)}, u32[]{:S(2)}, u32[]{:S(2)}) collective-permute-start(f32[128,8,128]{2,1,0:T(8,128)} %get-tuple-element.38), channel_id=1, source_target_pairs={{0,24},{8,0},{16,8},{24,16},{1,25},{9,1},{17,9},{25,17},{2,26},{10... | collective-permute-start | bytes 1572872 | tf_op jit(solution)/shard_map/ppermute | solution.py:332
  247.2 1.0 copy-start.4
  248.2 1.0 copy-start.6
  (4 other events, 3.5 us)
